TPU v7x, 512 devices: a whole 4x8x8 slice. The times are simulated.
512 devices in a mesh: ax: 16 (over y, core), th: 16 (over x_hi, z), grp: 2 (over x_lo).
Axes of the slice: x: 4 (x_hi: 2, x_lo: 2; x = x_hi * 2 + x_lo), y: 8, z: 8, core: 2. Of those that a mesh axis runs over, the one named last changes fastest.
Arguments:
- fields: float32 [4, 512, 384, 128], P(None, ('ax', 'grp'), 'th'), may hold values from -5 to 5, as said below
- wall_temp: float32 [512, 384, 64], P(('ax', 'grp'), 'th'), may hold values from -5 to 5
- fluid_metric: float32 [128], replicated, may hold values from 0.5 to 2
- fluid_radial_inverses: float32 [2, 128, 128], replicated, may hold values from 0 to 1, as said below
- wall_metric: float32 [64], replicated, may hold values from 0.5 to 2
- wall_inverse: float32 [64, 64], replicated, may hold values from 0 to 1, as said below
Outputs:
- predicted_coolant_state: float32 [4, 512, 384, 128], P(None, ('ax', 'grp'), 'th')
- new_wall: float32 [512, 384, 64], P(('ax', 'grp'), 'th')
Inputs may be any that keep to these rules, and one draw needn't show every extreme that they name: `fields`: components in the order axial, circumferential, radial velocity, temperature. fluid_radial_inverses[0] and fluid_radial_inverses[1] are the inverses of I - 0.4 L and I - 0.6 L with (L v)_j = m_j (e_j (v_(j+1) - v_j) - e_(j-1) (v_j - v_(j-1))), m = fluid_metric, e_j = (m_j + m_(j+1)) / 2 for j < 127, e_(127) = m_(127), e_(-1) = 0 and v_128 = 0. wall_inverse is the inverse of I - 0.8 L with L built as for the fluid from m = wall_metric, but e_(-1) = m_0, v_(-1) = 0 and e_(63) = 0.
All inputs are finite; a program needn't handle non-finite values.
Results may differ from a plain program's by a relative error of at most 0.00035.
Values sent between devices are 32-bit elements; how exact they have to be, the bound alone decides.
A program may use at most 64 MiB of HBM per device.

v0:
```python
import math

import jax
import jax.numpy as jnp
from jax import lax
from jax.sharding import PartitionSpec as P

X = 512
THETA = 384


EXACT_PRECISION = lax.Precision.HIGHEST
ADVECT_X = 0.08
ADVECT_T = 0.08
ADVECT_R = 0.15
LATERAL_U = 0.03
LATERAL_T = 0.04
LATERAL_W = 0.1
COUPLE_T = 0.6
COUPLE_W = 0.8


def tables(points):
    positions = jnp.arange(points)
    offset = positions[:, None] - positions[None, :]
    spacing = 2.0 * math.pi / points
    parity = (1 - 2 * (offset % 2)).astype(jnp.float32)
    nonzero = offset != 0
    polar_azimuths = jnp.where(nonzero, offset.astype(jnp.float32) * (0.5 * spacing), 1.0)
    first_table = jnp.where(nonzero, 0.5 * spacing * parity / jnp.tan(polar_azimuths), 0.0)
    second = jnp.where(
        nonzero,
        -parity * spacing * spacing / (2.0 * jnp.sin(polar_azimuths) ** 2),
        -(math.pi**2 / 3.0 + spacing * spacing / 6.0),
    )
    return jnp.concatenate([first_table, second], axis=0)


def fluid_radius(metric):
    spread = 1.0 / metric
    spread_total = jnp.sum(spread)
    beyond = jnp.cumsum(spread[::-1])[::-1]
    return 1.0 - 0.5 * (beyond - 0.5 * spread) / spread_total


def shell_distance_centre(metric):
    spread = 1.0 / metric
    spread_total = jnp.sum(spread)
    return 1.0 + 0.2 * (jnp.cumsum(spread) - 0.5 * spread) / spread_total


def shards(fields, wall_temp, fluid_metric, fluid_radial_inverses, wall_metric, wall_inverse):
    axial_lookup_table = tables(X)
    circle_table = tables(THETA)
    radius = fluid_radius(fluid_metric)
    wall_rad = shell_distance_centre(wall_metric)
    comps, x_local, t_local, r_all = fields.shape
    rw_all = wall_temp.shape[2]
    lateral_four = jnp.array([LATERAL_U, LATERAL_U, LATERAL_U, LATERAL_T], jnp.float32)
    th_count = lax.axis_size("th")
    r_circ = r_all // th_count
    w_circ = rw_all // th_count
    fluid_cols = comps * x_local * r_circ
    packed = jnp.concatenate(
        [
            fields.reshape(comps, x_local, t_local, th_count, r_circ)
            .transpose(2, 3, 0, 1, 4)
            .reshape(t_local, th_count, fluid_cols),
            wall_temp.reshape(x_local, t_local, th_count, w_circ)
            .transpose(1, 2, 0, 3)
            .reshape(t_local, th_count, x_local * w_circ),
        ],
        axis=2,
    )
    circle_in = lax.all_to_all(packed, "th", split_axis=1, concat_axis=0, tiled=True)
    circle_in = circle_in.reshape(circle_in.shape[0], circle_in.shape[2])
    t_whole = circle_in.shape[0]
    th_index = lax.axis_index("th")
    fluid_part = lax.dynamic_slice_in_dim(radius, th_index * r_circ, r_circ)
    wall_part = lax.dynamic_slice_in_dim(wall_rad, th_index * w_circ, w_circ)
    circle_derived = jnp.dot(
        circle_table, circle_in, precision=EXACT_PRECISION, preferred_element_type=jnp.float32
    )
    circle_first = circle_derived[:t_whole, :fluid_cols].reshape(t_whole, comps, x_local, r_circ)
    circle_second = circle_derived[t_whole:, :fluid_cols].reshape(t_whole, comps, x_local, r_circ)
    swirl = circle_in[:, x_local * r_circ : 2 * x_local * r_circ].reshape(
        t_whole, 1, x_local, r_circ
    )
    lat_circle = lateral_four[None, :, None, None]
    circle_fluid = (
        (-ADVECT_T * swirl * circle_first + lat_circle * circle_second / fluid_part) / fluid_part
    ).reshape(t_whole, fluid_cols)
    circle_wallterm = (
        LATERAL_W
        * circle_derived[t_whole:, fluid_cols:].reshape(t_whole, x_local, w_circ)
        / (wall_part * wall_part)
    ).reshape(t_whole, x_local * w_circ)
    azimuthal_bundle = jnp.concatenate([circle_fluid, circle_wallterm], axis=1)
    azimuthal_bundle = azimuthal_bundle.reshape(
        azimuthal_bundle.shape[0], 1, azimuthal_bundle.shape[1]
    )
    circle_home = lax.all_to_all(azimuthal_bundle, "th", split_axis=0, concat_axis=1, tiled=True)
    circle_terms = (
        circle_home[:, :, :fluid_cols]
        .reshape(t_local, th_count, comps, x_local, r_circ)
        .transpose(2, 3, 0, 1, 4)
        .reshape(comps, x_local, t_local, r_all)
    )
    circle_wall = (
        circle_home[:, :, fluid_cols:]
        .reshape(t_local, th_count, x_local, w_circ)
        .transpose(2, 0, 1, 3)
        .reshape(x_local, t_local, rw_all)
    )
    ax_count = lax.axis_size("ax")
    grp_count = lax.axis_size("grp")
    blocks = ax_count * grp_count
    lengthwise_coordinate = r_all // blocks
    w_axial = rw_all // blocks
    comp_cols = t_local * lengthwise_coordinate
    axial_cols = comps * comp_cols
    lengthwise_bundle = jnp.concatenate(
        [
            fields.reshape(comps, x_local, t_local, blocks, lengthwise_coordinate)
            .transpose(1, 3, 0, 2, 4)
            .reshape(x_local, blocks, axial_cols),
            wall_temp.reshape(x_local, t_local, blocks, w_axial)
            .transpose(0, 2, 1, 3)
            .reshape(x_local, blocks, t_local * w_axial),
        ],
        axis=2,
    )
    width = lengthwise_bundle.shape[2]
    axial_in = lax.all_to_all(
        lengthwise_bundle, ("ax", "grp"), split_axis=1, concat_axis=0, tiled=True
    )
    axial_in = axial_in.reshape(x_local * blocks, width)
    x_whole = axial_in.shape[0]
    axial_derived = jnp.dot(
        axial_lookup_table, axial_in, precision=EXACT_PRECISION, preferred_element_type=jnp.float32
    )
    stream = axial_in[:, :comp_cols].reshape(x_whole, 1, comp_cols)
    lat_axial = lateral_four[None, :, None]
    axial_fluid = -ADVECT_X * stream * axial_derived[:x_whole, :axial_cols].reshape(
        x_whole, comps, comp_cols
    ) + lat_axial * axial_derived[x_whole:, :axial_cols].reshape(x_whole, comps, comp_cols)
    axial_wallterm = LATERAL_W * axial_derived[x_whole:, axial_cols:]
    axial_out = jnp.concatenate([axial_fluid.reshape(x_whole, axial_cols), axial_wallterm], axis=1)
    axial_home = lax.all_to_all(
        axial_out.reshape(x_whole, 1, width), ("ax", "grp"), split_axis=0, concat_axis=1, tiled=True
    )
    axial_terms = (
        axial_home[:, :, :axial_cols]
        .reshape(x_local, blocks, comps, t_local, lengthwise_coordinate)
        .transpose(2, 0, 3, 1, 4)
        .reshape(comps, x_local, t_local, r_all)
    )
    axial_wall = (
        axial_home[:, :, axial_cols:]
        .reshape(x_local, blocks, t_local, w_axial)
        .transpose(0, 2, 1, 3)
        .reshape(x_local, t_local, rw_all)
    )
    ghost_wall = wall_temp[:, :, 0]
    fluid_last = fields[3, :, :, -1]
    ghosts = jnp.concatenate(
        [jnp.zeros((3,) + ghost_wall.shape + (1,), jnp.float32), ghost_wall[None, :, :, None]],
        axis=0,
    )
    upper_cells = jnp.concatenate([fields[:, :, :, 1:], ghosts], axis=3)
    lower_cells = jnp.concatenate([fields[:, :, :, :1], fields[:, :, :, :-1]], axis=3)
    radial_terms = -ADVECT_R * fields[2] * fluid_metric * (upper_cells - lower_cells) * 0.5
    right_side = fields + axial_terms + circle_terms + radial_terms
    fluid_lift = COUPLE_T * fluid_metric[-1] * fluid_metric[-1] * ghost_wall
    right_side = right_side.at[3, :, :, r_all - 1].add(fluid_lift)
    inverse_stack = fluid_radial_inverses[jnp.array([0, 0, 0, 1], jnp.int32)]
    predicted_coolant_state = jnp.einsum(
        "cij,cxtj->cxti", inverse_stack, right_side, precision=EXACT_PRECISION
    )
    first_cell = jnp.arange(rw_all) == 0
    wall_lift = COUPLE_W * wall_metric[0] * wall_metric[0] * fluid_last
    wall_side = (
        wall_temp + axial_wall + circle_wall + jnp.where(first_cell, wall_lift[:, :, None], 0.0)
    )
    new_wall = jnp.einsum("by,ldy->ldb", wall_inverse, wall_side, precision=EXACT_PRECISION)
    return (predicted_coolant_state, new_wall)


def solution(mesh):
    in_specs = (
        P(None, ("ax", "grp"), "th", None),
        P(("ax", "grp"), "th", None),
        P(),
        P(),
        P(),
        P(),
    )
    out_specs = (P(None, ("ax", "grp"), "th", None), P(("ax", "grp"), "th", None))
    return jax.shard_map(shards, mesh=mesh, in_specs=in_specs, out_specs=out_specs, check_vma=False)
```

profile of v0, /device:TPU:1, one launch (start us, length us, event | category | flops | bytes accessed | tf_op | source)
XLA Modules:
  0.0 180.4 jit_solution(16094459468582271989)
XLA Ops:
  2.4 2.6 %copy.206 = f32[4,16,24,128]{2,3,1,0:T(8,128)} copy(f32[4,16,24,128]{3,2,1,0:T(8,128)S(1)} %copy-done.1) | data formatting | bytes 1572864 | tf_op args[0]
  5.1 2.7 %copy.207 = f32[24,16,4,16,8]{0,4,3,2,1:T(8,128)S(1)} copy(f32[24,16,4,16,8]{0,4,1,3,2:T(8,128)} %bitcast.99) | data formatting | bytes 1572864 | tf_op jit(solution)/shard_map/transpose | solution.py:67
  7.8 2.5 %pad_maximum_fusion = f32[24,16,576]{0,2,1:T(8,128)} fusion(f32[24,16,64]{0,2,1:T(8,128)S(1)} %copy.210, f32[24,16,512]{0,2,1:T(8,128)S(1)} %bitcast.96), kind=kLoop, calls=%fused_computation.1 | loop fusion | flops 221184 | bytes 1769472 | tf_op jit(solution)/shard_map/concatenate | solution.py:64
  10.3 3.9 %copy.211 = f32[24,16,576]{2,0,1:T(8,128)} copy(f32[24,16,576]{0,2,1:T(8,128)} %pad_maximum_fusion) | data formatting | bytes 1769472 | tf_op jit(solution)/shard_map/concatenate | solution.py:64
  14.2 13.6 %all-to-all-start.2 = ((f32[24,16,576]{2,0,1:T(8,128)}), f32[24,16,576]{2,0,1:T(8,128)S(1)}, u32[]{:S(2)}, u32[]{:S(2)}) async-start(f32[24,16,576]{2,0,1:T(8,128)} %copy.211), calls=%async_computation.2 | async-start | bytes 1966080 | tf_op jit(solution)/shard_map/all_to_all | solution.py:75
  27.8 2.8 %copy.196 = f32[4,16,24,128]{2,1,3,0:T(8,128)} copy(f32[4,16,24,128]{3,2,1,0:T(8,128)S(1)} %copy-done.1) | data formatting | bytes 1572864 | tf_op args[0]
  33.1 5.9 %copy.197 = f32[16,32,4,24,4]{1,0,4,3,2:T(8,128)} copy(f32[16,32,4,24,4]{3,0,4,1,2:T(8,128)} %bitcast.94) | data formatting | bytes 1572864 | tf_op jit(solution)/shard_map/transpose | solution.py:125
  39.1 3.9 %pad_maximum_fusion.1 = f32[16,32,432]{1,0,2:T(8,128)} fusion(f32[16,32,48]{1,0,2:T(8,128)S(1)} %bitcast.114, f32[16,32,384]{1,0,2:T(8,128)} %bitcast.100), kind=kLoop, calls=%fused_computation.3 | loop fusion | flops 221184 | bytes 1769472 | tf_op jit(solution)/shard_map/concatenate | solution.py:122
  43.0 3.8 %copy.200 = f32[16,32,432]{2,0,1:T(8,128)} copy(f32[16,32,432]{1,0,2:T(8,128)} %pad_maximum_fusion.1) | data formatting | bytes 1769472 | tf_op jit(solution)/shard_map/concatenate | solution.py:122
  46.8 6.6 %all-to-all-done.2 = f32[24,16,576]{2,0,1:T(8,128)S(1)} async-done(((f32[24,16,576]{2,0,1:T(8,128)}), f32[24,16,576]{2,0,1:T(8,128)S(1)}, u32[]{:S(2)}, u32[]{:S(2)}) %all-to-all-start.2) | async-done | bytes 884768 | tf_op jit(solution)/shard_map/all_to_all | solution.py:75
  53.5 9.8 %all-to-all-start = ((f32[16,32,432]{2,0,1:T(8,128)}), f32[16,32,432]{2,0,1:T(8,128)S(1)}, u32[]{:S(2)}, u32[]{:S(2)}) async-start(f32[16,32,432]{2,0,1:T(8,128)} %copy.200), calls=%async_computation | async-start | bytes 2097152 | tf_op jit(solution)/shard_map/all_to_all | solution.py:134
  67.3 3.5 %divide_select_fusion.2 = (f32[384,384]{1,0:T(8,128)}, f32[384,384]{1,0:T(8,128)}) fusion(), kind=kLoop, calls=%fused_computation.50 | loop fusion | flops 4128768 | bytes 1179648 | tf_op jit(solution)/shard_map/jit(_where)/select_n | solution.py:31
  73.2 4.4 %fusion.4 = f32[768,576]{0,1:T(8,128)S(1)} fusion(f32[384,576]{1,0:T(8,128)S(1)} %bitcast.107, f32[384,384]{1,0:T(8,128)} %get-tuple-element.21, f32[384,384]{1,0:T(8,128)} %get-tuple-element.22), kind=kOutput, calls=%fused_computation.11 | convolution fusion | flops 2038726656 | bytes 3833856 | tf_op jit(solution)/shard_map/dot_general | solution.py:81
  78.0 1.9 %copy.215 = f32[384,1,576]{2,1,0:T(1,128)} copy(f32[384,1,576]{0,2,1:T(8,128)S(1)} %maximum_bitcast_fusion.1) | data formatting | bytes 1769472 | tf_op jit(solution)/shard_map/reshape | solution.py:99
  79.9 11.8 %all-to-all-done = f32[16,32,432]{2,0,1:T(8,128)S(1)} async-done(((f32[16,32,432]{2,0,1:T(8,128)}), f32[16,32,432]{2,0,1:T(8,128)S(1)}, u32[]{:S(2)}, u32[]{:S(2)}) %all-to-all-start) | async-done | bytes 884768 | tf_op jit(solution)/shard_map/all_to_all | solution.py:134
  91.7 4.7 %all-to-all-start.3 = ((f32[384,1,576]{2,1,0:T(1,128)}), f32[384,1,576]{2,1,0:T(1,128)}, u32[]{:S(2)}, u32[]{:S(2)}) async-start(f32[384,1,576]{2,1,0:T(1,128)} %copy.215), calls=%async_computation.3 | async-start | bytes 1966080 | tf_op jit(solution)/shard_map/all_to_all | solution.py:102
  96.6 5.6 %divide_select_fusion = (f32[512,512]{1,0:T(8,128)S(1)}, f32[512,512]{1,0:T(8,128)}) fusion(), kind=kLoop, calls=%fused_computation.19 | loop fusion | flops 7340032 | bytes 2097152 | tf_op jit(solution)/shard_map/jit(_where)/select_n | solution.py:31
  105.7 4.2 %fusion = f32[1024,432]{0,1:T(8,128)S(1)} fusion(f32[512,432]{1,0:T(8,128)S(1)} %bitcast.105, f32[512,512]{1,0:T(8,128)S(1)} %get-tuple-element.23, f32[512,512]{1,0:T(8,128)} %get-tuple-element.24), kind=kOutput, calls=%fused_computation.4 | convolution fusion | flops 2718433280 | bytes 4751360 | tf_op jit(solution)/shard_map/dot_general | solution.py:139
  110.2 2.0 %copy.202 = f32[512,1,432]{2,1,0:T(1,128)} copy(f32[512,1,432]{0,2,1:T(8,128)S(1)} %maximum_bitcast_fusion) | data formatting | bytes 1769472 | tf_op jit(solution)/shard_map/reshape | solution.py:150
  112.2 10.0 %all-to-all-done.3 = f32[384,1,576]{2,1,0:T(1,128)} async-done(((f32[384,1,576]{2,1,0:T(1,128)}), f32[384,1,576]{2,1,0:T(1,128)}, u32[]{:S(2)}, u32[]{:S(2)}) %all-to-all-start.3) | async-done | bytes 884768 | tf_op jit(solution)/shard_map/all_to_all | solution.py:102
  122.2 6.1 %all-to-all-start.1 = ((f32[512,1,432]{2,1,0:T(1,128)}), f32[512,1,432]{2,1,0:T(1,128)S(1)}, u32[]{:S(2)}, u32[]{:S(2)}) async-start(f32[512,1,432]{2,1,0:T(1,128)} %copy.202), calls=%async_computation.1 | async-start | bytes 2097152 | tf_op jit(solution)/shard_map/all_to_all | solution.py:149
  136.6 2.0 %copy.225 = f32[24,16,64]{0,1,2:T(8,128)} copy(f32[24,16,64]{2,0,1:T(8,128)} %slice.128) | data formatting | bytes 196608 | tf_op jit(solution)/shard_map/slice | solution.py:110
  138.5 2.2 %copy.226 = f32[16,24,16,4]{1,0,3,2:T(8,128)} copy(f32[16,24,16,4]{1,2,3,0:T(8,128)} %bitcast.112) | data formatting | bytes 196608 | tf_op jit(solution)/shard_map/transpose | solution.py:112
  140.7 2.6 %copy.216 = f32[24,16,512]{0,2,1:T(8,128)} copy(f32[24,16,512]{2,0,1:T(8,128)S(1)} %slice.124) | data formatting | bytes 1572864 | tf_op jit(solution)/shard_map/slice | solution.py:104
  143.3 4.7 %copy.236 = f32[4,16,24,16,8]{2,4,3,1,0:T(8,128)} copy(f32[4,16,24,16,8]{2,4,1,0,3:T(8,128)} %bitcast.97) | data formatting | bytes 1572864 | tf_op jit(solution)/shard_map/transpose | solution.py:106
  148.1 2.8 %copy.218 = f32[4,16,24,128]{3,2,1,0:T(8,128)S(1)} copy(f32[4,16,24,128]{2,3,1,0:T(8,128)} %bitcast.98) | data formatting | bytes 1572864 | tf_op jit(solution)/shard_map/reshape | solution.py:107
  150.9 6.0 %all-to-all-done.1 = f32[512,1,432]{2,1,0:T(1,128)S(1)} async-done(((f32[512,1,432]{2,1,0:T(1,128)}), f32[512,1,432]{2,1,0:T(1,128)S(1)}, u32[]{:S(2)}, u32[]{:S(2)}) %all-to-all-start.1) | async-done | bytes 884768 | tf_op jit(solution)/shard_map/all_to_all | solution.py:149
  158.0 2.2 %copy.223 = f32[16,24,32,2]{1,0,3,2:T(8,128)} copy(f32[16,24,32,2]{2,0,3,1:T(8,128)} %bitcast.115) | data formatting | bytes 196608 | tf_op jit(solution)/shard_map/transpose | solution.py:161
  160.2 2.2 %copy.203 = f32[16,32,384]{1,0,2:T(8,128)} copy(f32[16,32,384]{2,0,1:T(8,128)S(1)} %slice.119) | data formatting | bytes 1572864 | tf_op jit(solution)/shard_map/slice | solution.py:153
  162.4 6.2 %copy.204 = f32[4,16,24,32,4]{2,1,4,3,0:T(8,128)} copy(f32[4,16,24,32,4]{3,1,4,2,0:T(8,128)} %bitcast.101) | data formatting | bytes 1572864 | tf_op jit(solution)/shard_map/transpose | solution.py:155
  168.7 3.0 %copy.205 = f32[4,16,24,128]{3,2,1,0:T(8,128)S(1)} copy(f32[4,16,24,128]{2,1,3,0:T(8,128)} %bitcast.95) | data formatting | bytes 1572864 | tf_op jit(solution)/shard_map/reshape | solution.py:156
  177.7 2.7 %fusion.35 = f32[4,16,24,128]{3,2,1,0:T(8,128)} fusion(f32[4,16,24,128]{3,2,1,0:T(8,128)S(1)} %scatter-add.4, f32[4,128,128]{2,1,0:T(8,128)} %gather_fusion), kind=kOutput, calls=%fused_computation.63 | convolution fusion | flops 301989888 | bytes 1835008 | tf_op jit(solution)/shard_map/cij,cxtj->cxti/dot_general | solution.py:177
  (83 shorter events, 28.9 us)
Async XLA Ops:
  0.6 129.8 %copy-start = (f32[2,128,128]{2,1,0:T(8,128)S(1)}, f32[2,128,128]{2,1,0:T(8,128)}, u32[]{:S(2)}) copy-start(f32[2,128,128]{2,1,0:T(8,128)} %param.13) | copy-start | bytes 393220
  0.6 1.8 copy-start.1
  14.2 16.4 %copy-start.8 = (f32[128]{0:T(128)S(1)}, f32[128]{0:T(128)}, u32[]{:S(2)}) copy-start(f32[128]{0:T(128)} %param.12) | copy-start | bytes 1540
  14.2 16.5 %copy-start.10 = (f32[64]{0:T(128)S(1)}, f32[64]{0:T(128)}, u32[]{:S(2)}) copy-start(f32[64]{0:T(128)} %param.14) | copy-start | bytes 772
  14.2 18.3 %copy-start.6 = (f32[4]{0:T(128)S(1)}, f32[4]{0:T(128)}, u32[]{:S(2)}) copy-start(f32[4]{0:T(128)} %constant.132.clone) | copy-start | bytes 52
  14.2 39.2 %all-to-all-start.2 = ((f32[24,16,576]{2,0,1:T(8,128)}), f32[24,16,576]{2,0,1:T(8,128)S(1)}, u32[]{:S(2)}, u32[]{:S(2)}) async-start(f32[24,16,576]{2,0,1:T(8,128)} %copy.211), calls=%async_computation.2 | async-start | bytes 1966080 | tf_op jit(solution)/shard_map/all_to_all | solution.py:75
  53.5 38.2 %all-to-all-start = ((f32[16,32,432]{2,0,1:T(8,128)}), f32[16,32,432]{2,0,1:T(8,128)S(1)}, u32[]{:S(2)}, u32[]{:S(2)}) async-start(f32[16,32,432]{2,0,1:T(8,128)} %copy.200), calls=%async_computation | async-start | bytes 2097152 | tf_op jit(solution)/shard_map/all_to_all | solution.py:134
  73.2 4.4 %copy-start.4 = (f32[384,128]{0,1:T(8,128)S(1)}, f32[384,128]{0,1:T(8,128)}, u32[]{:S(2)}) copy-start(f32[384,128]{0,1:T(8,128)} %copy.212) | copy-start | bytes 589828
  91.7 30.5 %all-to-all-start.3 = ((f32[384,1,576]{2,1,0:T(1,128)}), f32[384,1,576]{2,1,0:T(1,128)}, u32[]{:S(2)}, u32[]{:S(2)}) async-start(f32[384,1,576]{2,1,0:T(1,128)} %copy.215), calls=%async_computation.3 | async-start | bytes 1966080 | tf_op jit(solution)/shard_map/all_to_all | solution.py:102
  110.1 18.2 %copy-start.9 = (f32[128]{0:T(128)S(1)}, f32[128]{0:T(128)}, u32[]{:S(2)}) copy-start(f32[128]{0:T(128)} %param.12) | copy-start | bytes 1540
  110.1 20.1 %copy-start.11 = (f32[64]{0:T(128)S(1)}, f32[64]{0:T(128)}, u32[]{:S(2)}) copy-start(f32[64]{0:T(128)} %param.14) | copy-start | bytes 772
  110.1 20.4 %copy-start.7 = (s32[4]{0:T(128)S(1)}, s32[4]{0:T(128)}, u32[]{:S(2)}) copy-start(s32[4]{0:T(128)} %constant.142) | copy-start | bytes 52
  122.2 34.6 %all-to-all-start.1 = ((f32[512,1,432]{2,1,0:T(1,128)}), f32[512,1,432]{2,1,0:T(1,128)S(1)}, u32[]{:S(2)}, u32[]{:S(2)}) async-start(f32[512,1,432]{2,1,0:T(1,128)} %copy.202), calls=%async_computation.1 | async-start | bytes 2097152 | tf_op jit(solution)/shard_map/all_to_all | solution.py:149
  168.7 4.5 %copy-start.5 = (f32[64,64]{1,0:T(8,128)S(1)}, f32[64,64]{1,0:T(8,128)}, u32[]{:S(2)}) copy-start(f32[64,64]{1,0:T(8,128)} %param.15) | copy-start | bytes 49156
  171.7 3.2 %copy-start.2 = (f32[4,16,24,127]{3,2,1,0:T(8,128)S(1)}, f32[4,16,24,127]{3,2,1,0:T(8,128)}, u32[]{:S(2)}) copy-start(f32[4,16,24,127]{3,2,1,0:T(8,128)} %get-tuple-element.18) | copy-start | bytes 2340868
  171.7 3.2 %copy-start.3 = (f32[4,16,24,127]{3,2,1,0:T(8,128)S(1)}, f32[4,16,24,127]{3,2,1,0:T(8,128)}, u32[]{:S(2)}) copy-start(f32[4,16,24,127]{3,2,1,0:T(8,128)} %get-tuple-element.19) | copy-start | bytes 2340868
where the time goes:
time: 182 us; the launch traced here: 180 us
  local copies, waits for them, and re-layouts  69.7 us (38%)
  waiting for transfers between devices  34.4 us (19%)
  starting transfers between devices  34.2 us (19%)
  other arithmetic  26.7 us (15%)
  matrix products  13 us (7%)
  between operations  2.37 us (1%)
    all_to_all x1, starting transfers between devices, shards(): lax.all_to_all(packed, 'th', split_axis=1, concat_axis=0, tiled=True)  13.6 us
    all_to_all x1, waiting for transfers between devices, shards(): lax.all_to_all(lengthwise_bundle, ('ax', 'grp'), split_axis=1, concat_axi...  11.8 us
    all_to_all x1, waiting for transfers between devices, shards(): lax.all_to_all(azimuthal_bundle, 'th', split_axis=0, concat_axis=1, tiled...  10 us
    unnamed x30, local copies, waits for them, and re-layouts  9.89 us
    all_to_all x1, starting transfers between devices, shards(): lax.all_to_all(lengthwise_bundle, ('ax', 'grp'), split_axis=1, concat_axi...  9.79 us
    select_n x2, other arithmetic, tables(): jnp.where(nonzero, -parity * spacing * spacing / (2.0 * jnp.sin(polar_azi...  9.1 us
    all_to_all x1, waiting for transfers between devices, shards(): lax.all_to_all(packed, 'th', split_axis=1, concat_axis=0, tiled=True)  6.65 us
    transpose x2, local copies, waits for them, and re-layouts, shards(): lengthwise_bundle = jnp.concatenate([fields.reshape(comps, x_local, t_loc...  6.42 us
  transfers between devices with their start and end apart: 4, of which 4 were waited for; matrix products, arithmetic and copies ran while one was open for 40% of the time, Pallas kernels for 0%

commit v1 on v0

v1 whole, which is shorter than its diff:
```python
import functools

import jax
import jax.numpy as jnp
import numpy as np
from jax import lax
from jax.experimental import pallas as pl
from jax.experimental.pallas import tpu as pltpu
from jax.sharding import PartitionSpec as P

MESH = pl.DeviceIdType.MESH
F32 = jnp.float32
BF16 = jnp.bfloat16

X = 512
THETA = 384
R = 128
RW = 64
XL = 16
TL = 24
NT = 16
NA = 32

ADVECT_X = 0.08
ADVECT_T = 0.08
ADVECT_R = 0.15
LATERAL_U = 0.03
LATERAL_T = 0.04
LATERAL_W = 0.1
COUPLE_T = 0.6
COUPLE_W = 0.8


def folded_tables(points):
    spacing = 2.0 * np.pi / points
    offset = np.arange(points)[:, None] - np.arange(points)[None, :]
    parity = 1.0 - 2.0 * (offset % 2)
    angle = np.where(offset != 0, offset * 0.5 * spacing, 1.0)
    first = np.where(offset != 0, 0.5 * spacing * parity / np.tan(angle), 0.0)
    second = np.where(
        offset != 0,
        -parity * spacing**2 / (2.0 * np.sin(angle) ** 2),
        -(np.pi**2 / 3.0 + spacing**2 / 6.0),
    )
    half = points // 2
    parts = []
    for sign in (1.0, -1.0):
        both = np.concatenate(
            [0.5 * (table[:half, :half] + sign * table[:half, half:]) for table in (first, second)], axis=0
        ).astype(np.float32)
        high = both.astype(BF16)
        low = (both - high.astype(np.float32)).astype(BF16)
        parts.append(np.stack([high, low]))
    return np.stack(parts)


def split(value):
    high = value.astype(BF16)
    low = (value - high.astype(F32)).astype(BF16)
    return high, low


def dot(a, b):
    return jnp.dot(a, b, preferred_element_type=F32)


def dot_t(a, b):
    return lax.dot_general(a, b, (((1,), (1,)), ((), ())), preferred_element_type=F32)


def apply_folded(table, rows, top, bottom):
    results = []
    for which, value in ((0, top + bottom), (1, top - bottom)):
        high, low = split(value)
        t_high = table[which, 0, rows, :]
        t_low = table[which, 1, rows, :]
        results.append(dot(t_high, high) + dot(t_high, low) + dot(t_low, high))
    return results[0] + results[1], results[0] - results[1]


def kernel(
    fields_h, wall_h, fm, inv, wm, winv, ttab_h, xtab_h,
    out_h, wout_h,
    F, W, ttab, xtab,
    fT, WP, wT,
    Qt, Qx, Wt, Wx,
    Rt, Rx, WRt, WRx, Wn,
    cih, axh, cwh, awh,
    base, wbase, obuf, wobuf,
    ld, st,
    sT, rT, sX, rX, sWT, rWT, sWX, rWX,
    bsT, brT, bsX, brX, bsWT, brWT, bsWX, brWX,
):
    ax = lax.axis_index("ax")
    th = lax.axis_index("th")
    grp = lax.axis_index("grp")
    a = ax * 2 + grp
    y = lax.div(ax, 2)
    core = lax.rem(ax, 2)
    xh = lax.div(th, 8)
    z = lax.rem(th, 8)
    odd_y = lax.rem(y, 2)
    x_wall = jnp.logical_and(core == 0, grp == odd_y)
    x_fluid = jnp.logical_not(x_wall)
    my_theta = 3 * y + core * (1 + grp)
    t_wall = xh == lax.rem(z, 2)

    barrier = pltpu.get_barrier_semaphore()

    def greet_t(k, _):
        pl.semaphore_signal(barrier, inc=1, device_id=(ax, lax.rem(th + k, NT), grp), device_id_type=MESH)
        return 0

    def greet_a(k, _):
        peer = lax.rem(a + k, NA)
        pl.semaphore_signal(
            barrier, inc=1, device_id=(lax.div(peer, 2), th, lax.rem(peer, 2)), device_id_type=MESH
        )
        return 0

    lax.fori_loop(1, NT, greet_t, 0)
    lax.fori_loop(1, NA, greet_a, 0)

    load_f = pltpu.make_async_copy(fields_h, F, ld.at[0])
    load_w = pltpu.make_async_copy(wall_h, W, ld.at[1])
    load_t = pltpu.make_async_copy(ttab_h, ttab, ld.at[2])
    load_x = pltpu.make_async_copy(xtab_h, xtab, ld.at[3])
    load_f.start()
    load_w.start()
    load_t.start()
    load_x.start()
    load_f.wait()

    F2 = F.reshape(4 * XL * TL, R)

    def turn(t, _):
        for c in range(4):
            fT[c // 2, t, c % 2] = F2[pl.ds(c * XL * TL + t, XL, stride=TL), :]
        return 0

    lax.fori_loop(0, TL, turn, 0)
    load_w.wait()
    for p in range(8):
        WP[p] = jnp.concatenate([W[p], W[p + 8]], axis=1)
    WP2 = WP.reshape(8 * TL, R)
    for t in range(TL):
        wT[t] = WP2[pl.ds(t, 8, stride=TL), :]

    pl.semaphore_wait(barrier, NT - 1 + NA - 1)

    def offset(i):
        return 4 + lax.div(i + 1, 2) * (1 - 2 * lax.rem(i, 2))

    def send(remote, src, dst, s_sem, r_sem, device):
        @pl.when(remote)
        def _():
            pltpu.make_async_remote_copy(
                src_ref=src, dst_ref=dst, send_sem=s_sem, recv_sem=r_sem, device_id=device, device_id_type=MESH
            ).start()

        @pl.when(jnp.logical_not(remote))
        def _():
            pltpu.make_async_copy(src, dst, r_sem).start()

    def theta_peer(i, flip):
        return lax.rem(xh + flip, 2) * 8 + lax.rem(z + offset(i), 8)

    def send_chunk(ch):
        def step(i, _):
            for flip in (1, 0):
                t = theta_peer(i, flip)
                send(
                    t != th, F.at[pl.ds(2 * ch, 2), t], Qt.at[pl.ds(2 * ch, 2), pl.ds(TL * th, TL)],
                    sT.at[ch], rT.at[ch], (ax, t, grp),
                )
            yy = lax.rem(y + offset(i), 8)
            for k in range(3):
                theta = 3 * yy + k
                c_to = (k + 1) // 2
                g_to = k // 2 + (1 - c_to) * (1 - lax.rem(yy, 2))
                a_to = 4 * yy + 2 * c_to + g_to
                send(
                    a_to != a, fT.at[ch, theta], Qx.at[pl.ds(2 * ch, 2), pl.ds(XL * a, XL)],
                    sX.at[ch], rX.at[ch], (2 * yy + c_to, th, g_to),
                )
            return 0

        lax.fori_loop(0, 8, step, 0)

    def send_wall():
        def step(i, _):
            p = lax.rem(z + offset(i), 8)
            t = lax.rem(p, 2) * 8 + p
            send(t != th, WP.at[p], Wt.at[pl.ds(TL * th, TL)], sWT, rWT, (ax, t, grp))
            yy = lax.rem(y + offset(i), 8)
            a_to = 4 * yy + lax.rem(yy, 2)
            send(
                a_to != a, wT.at[pl.ds(3 * yy, 3)], Wx.at[:, pl.ds(8 * a, 8)],
                sWX, rWX, (2 * yy, th, lax.rem(yy, 2)),
            )
            return 0

        lax.fori_loop(0, 8, step, 0)

    send_chunk(0)
    send_wall()
    send_chunk(1)

    lane = lax.broadcasted_iota(jnp.int32, (TL, R), 1)
    m = fm[...]
    row_r = -0.5 * ADVECT_R * m
    row_lift = COUPLE_T * m * m
    wm2 = jnp.concatenate([wm[...], wm[...]], axis=1)
    row_wlift = COUPLE_W * wm2 * wm2

    kk = lax.broadcasted_iota(jnp.int32, (R, R), 0)
    jj = lax.broadcasted_iota(jnp.int32, (R, R), 1)
    spread = 1.0 / m
    spread_t = jnp.broadcast_to(spread, (R, R)).T
    beyond = jnp.sum(jnp.where(kk >= jj, spread_t, 0.0), axis=0, keepdims=True)
    total = jnp.sum(spread_t, axis=0, keepdims=True)
    radius = 1.0 - 0.5 * (beyond - 0.5 * spread) / total
    row_t1 = -ADVECT_T / radius
    row_t2 = 1.0 / (radius * radius)
    wspread = 1.0 / wm2
    wspread_t = jnp.broadcast_to(wspread, (R, R)).T
    within = jnp.sum(jnp.where(kk <= lax.rem(jj, RW), wspread_t, 0.0), axis=0, keepdims=True)
    wtotal = jnp.sum(jnp.where(kk < RW, wspread_t, 0.0), axis=0, keepdims=True)
    wradius = 1.0 + 0.2 * (within - 0.5 * wspread) / wtotal
    row_w2 = LATERAL_W / (wradius * wradius)

    def prepare(p, _):
        pair = WP[p]
        for h in range(2):
            x = p + 8 * h
            u_r = F[2, x] * row_r
            ghost = pltpu.roll(pair, 127 - 64 * h, axis=1)
            for c in range(4):
                q = F[c, x]
                edge = ghost if c == 3 else 0.0
                upper = jnp.where(lane == R - 1, edge, pltpu.roll(q, R - 1, axis=1))
                lower = jnp.where(lane == 0, q, pltpu.roll(q, 1, axis=1))
                value = q + u_r * (upper - lower)
                if c == 3:
                    value = value + jnp.where(lane == R - 1, row_lift * ghost, 0.0)
                base[c, x] = value
        last_0 = pltpu.roll(F[3, p], 1, axis=1)
        last_1 = pltpu.roll(F[3, p + 8], 65, axis=1)
        wbase[p] = pair + jnp.where(
            lane == 0, row_wlift * last_0, jnp.where(lane == RW, row_wlift * last_1, 0.0)
        )
        return 0

    lax.fori_loop(0, 8, prepare, 0)
    load_t.wait()
    load_x.wait()

    def full(ref, sem):
        pltpu.make_async_copy(ref, ref, sem).wait()

    half_t = THETA // 2
    half_x = X // 2

    def lam(ch, cc):
        return jnp.where(ch == 1, LATERAL_T, LATERAL_U) if cc == 1 else LATERAL_U

    def theta_chunk(ch):
        both = pl.ds(2 * ch, 2)
        full(Qt.at[both], rT.at[ch])
        top = jnp.concatenate([Qt[2 * ch, :half_t], Qt[2 * ch + 1, :half_t]], axis=1)
        bottom = jnp.concatenate([Qt[2 * ch, half_t:], Qt[2 * ch + 1, half_t:]], axis=1)
        firsts = apply_folded(ttab, slice(0, half_t), top, bottom)
        seconds = apply_folded(ttab, slice(half_t, THETA), top, bottom)
        for h in range(2):
            rows = slice(h * half_t, (h + 1) * half_t)
            swirl = Qt[1, rows] * row_t1
            for cc in range(2):
                cols = slice(cc * R, (cc + 1) * R)
                Rt[2 * ch + cc, rows] = swirl * firsts[h][:, cols] + seconds[h][:, cols] * (row_t2 * lam(ch, cc))

        def step(i, _):
            for flip in (1, 0):
                t = theta_peer(i, flip)
                send(
                    t != th, Rt.at[both, pl.ds(TL * t, TL)], cih.at[both, th], bsT.at[ch], brT.at[ch], (ax, t, grp)
                )
            return 0

        lax.fori_loop(0, 8, step, 0)

    def axial_chunk(ch):
        both = pl.ds(2 * ch, 2)
        full(Qx.at[both], rX.at[ch])
        top = jnp.concatenate([Qx[2 * ch, :half_x], Qx[2 * ch + 1, :half_x]], axis=1)
        bottom = jnp.concatenate([Qx[2 * ch, half_x:], Qx[2 * ch + 1, half_x:]], axis=1)
        firsts = apply_folded(xtab, slice(0, half_x), top, bottom)
        seconds = apply_folded(xtab, slice(half_x, X), top, bottom)
        for h in range(2):
            rows = slice(h * half_x, (h + 1) * half_x)
            stream = Qx[0, rows] * (-ADVECT_X)
            for cc in range(2):
                cols = slice(cc * R, (cc + 1) * R)
                Rx[2 * ch + cc, rows] = stream * firsts[h][:, cols] + seconds[h][:, cols] * lam(ch, cc)

        def step(i, _):
            yy = lax.rem(y + offset(i), 8)
            for k in range(4):
                a_to = 4 * yy + k
                send(
                    a_to != a, Rx.at[both, pl.ds(XL * a_to, XL)], axh.at[ch, my_theta],
                    bsX.at[ch], brX.at[ch], (2 * yy + k // 2, th, k % 2),
                )
            return 0

        lax.fori_loop(0, 8, step, 0)

    def theta_wall():
        full(Wt, rWT)
        seconds = apply_folded(ttab, slice(half_t, THETA), Wt[:half_t], Wt[half_t:])
        for h in range(2):
            WRt[h * half_t:(h + 1) * half_t] = seconds[h] * row_w2

        def step(i, _):
            for flip in (1, 0):
                t = theta_peer(i, flip)
                send(t != th, WRt.at[pl.ds(TL * t, TL)], cwh.at[z], bsWT, brWT, (ax, t, grp))
            return 0

        lax.fori_loop(0, 8, step, 0)

    low8 = lax.broadcasted_iota(jnp.int32, (8, R), 1) < RW

    def axial_wall():
        full(Wx, rWX)

        def unpack(s, _):
            rows = pl.ds(pl.multiple_of(8 * s, 8), 8)
            w0, w1, w2 = Wx[0, rows], Wx[1, rows], Wx[2, rows]
            even = pl.ds(pl.multiple_of(16 * s, 8), 8)
            odd = pl.ds(pl.multiple_of(16 * s + 8, 8), 8)
            Wn[even, 0:R] = jnp.where(low8, w0, pltpu.roll(w1, RW, axis=1))
            Wn[odd, 0:R] = jnp.where(low8, pltpu.roll(w0, RW, axis=1), w1)
            Wn[even, R:2 * R] = w2
            Wn[odd, R:2 * R] = pltpu.roll(w2, RW, axis=1)
            return 0

        lax.fori_loop(0, NA, unpack, 0)
        seconds = apply_folded(xtab, slice(half_x, X), Wn[:half_x], Wn[half_x:])
        for h in range(2):
            Wn[h * half_x:(h + 1) * half_x] = seconds[h] * LATERAL_W

        def pack(s, _):
            rows = pl.ds(pl.multiple_of(8 * s, 8), 8)
            even = pl.ds(pl.multiple_of(16 * s, 8), 8)
            odd = pl.ds(pl.multiple_of(16 * s + 8, 8), 8)
            e01, o01 = Wn[even, 0:R], Wn[odd, 0:R]
            WRx[0, rows] = jnp.where(low8, e01, pltpu.roll(o01, RW, axis=1))
            WRx[1, rows] = jnp.where(low8, pltpu.roll(e01, RW, axis=1), o01)
            WRx[2, rows] = jnp.where(low8, Wn[even, R:2 * R], pltpu.roll(Wn[odd, R:2 * R], RW, axis=1))
            return 0

        lax.fori_loop(0, NA, pack, 0)

        def step(i, _):
            yy = lax.rem(y + offset(i), 8)
            for k in range(4):
                a_to = 4 * yy + k
                send(
                    a_to != a, WRx.at[:, pl.ds(8 * a_to, 8)], awh.at[pl.ds(3 * y, 3)],
                    bsWX, brWX, (2 * yy + k // 2, th, k % 2),
                )
            return 0

        lax.fori_loop(0, 8, step, 0)

    theta_chunk(0)
    pl.when(x_fluid)(lambda: axial_chunk(0))
    pl.when(x_wall)(axial_wall)
    pl.when(t_wall)(theta_wall)
    theta_chunk(1)
    pl.when(x_fluid)(lambda: axial_chunk(1))

    axh2 = axh.reshape(4 * XL * TL, R)

    def inverse_parts(matrix):
        high, low = split(matrix)
        return jnp.concatenate([high, high, low], axis=1)

    def value_parts(value):
        high, low = split(value)
        return jnp.concatenate([high, low, high], axis=1)

    def finish(ch):
        full(cih.at[pl.ds(2 * ch, 2)], brT.at[ch])
        full(axh.at[ch], brX.at[ch])
        for cc in range(2):
            c = 2 * ch + cc

            def gather(x, _):
                axial = axh2[pl.ds(ch * 2 * XL * TL + cc * XL + x, TL, stride=2 * XL), :]
                base[c, x] = base[c, x] + cih[c, x] + axial
                return 0

            lax.fori_loop(0, XL, gather, 0)
            matrix = inverse_parts(inv[1 if c == 3 else 0])
            value = value_parts(base[c].reshape(XL * TL, R))
            obuf[c] = dot_t(value, matrix).reshape(XL, TL, R)
            pltpu.make_async_copy(obuf.at[c], out_h.at[c], st.at[c]).start()

    finish(0)
    full(cwh, brWT)
    full(awh, brWX)
    awh2 = awh.reshape(8 * TL, R)

    def gather_wall(p, _):
        wbase[p] = wbase[p] + cwh[p] + awh2[pl.ds(p, TL, stride=8), :]
        return 0

    lax.fori_loop(0, 8, gather_wall, 0)
    value = value_parts(wbase[...].reshape(8 * TL, R))
    nothing = jnp.zeros((RW, RW), F32)
    for h in range(2):
        pair = [winv[...], nothing] if h == 0 else [nothing, winv[...]]
        matrix = inverse_parts(jnp.concatenate(pair, axis=1))
        wobuf[8 * h:8 * h + 8] = dot_t(value, matrix).reshape(8, TL, RW)
    pltpu.make_async_copy(wobuf, wout_h, st.at[4]).start()
    finish(1)

    for ch in range(2):
        full(F.at[pl.ds(0, 2), pl.ds(0, NT - 1)], sT.at[ch])
        full(F.at[pl.ds(0, 2), pl.ds(0, NT - 1)], bsT.at[ch])

        @pl.when(x_fluid)
        def _():
            full(fT.at[ch, pl.ds(0, TL - 1)], sX.at[ch])
            full(Rx.at[pl.ds(0, 2), pl.ds(0, X - XL)], bsX.at[ch])

        @pl.when(x_wall)
        def _():
            full(fT.at[ch], sX.at[ch])

    @pl.when(t_wall)
    def _():
        full(WP.at[pl.ds(0, 7)], sWT)
        full(WRt.at[pl.ds(0, THETA - TL)], bsWT)

    @pl.when(jnp.logical_not(t_wall))
    def _():
        full(WP, sWT)

    @pl.when(x_wall)
    def _():
        full(wT.at[pl.ds(0, TL - 3)], sWX)
        full(WRx.at[:, pl.ds(0, 8 * (NA - 1))], bsWX)

    @pl.when(x_fluid)
    def _():
        full(wT, sWX)

    for c in range(4):
        pltpu.make_async_copy(obuf.at[c], out_h.at[c], st.at[c]).wait()
    pltpu.make_async_copy(wobuf, wout_h, st.at[4]).wait()


def shards(fields, wall_temp, fluid_metric, fluid_radial_inverses, wall_metric, wall_inverse):
    vmem = pl.BlockSpec(memory_space=pltpu.VMEM)
    hbm = pl.BlockSpec(memory_space=pl.ANY)
    dma = pltpu.SemaphoreType.DMA
    ttab = jnp.asarray(folded_tables(THETA))
    xtab = jnp.asarray(folded_tables(X))

    def buf(*shape, dtype=F32):
        return pltpu.VMEM(shape, dtype)

    return pl.pallas_call(
        kernel,
        out_shape=(
            jax.ShapeDtypeStruct((4, XL, TL, R), F32),
            jax.ShapeDtypeStruct((XL, TL, RW), F32),
        ),
        in_specs=[hbm, hbm, vmem, vmem, vmem, vmem, hbm, hbm],
        out_specs=(hbm, hbm),
        scratch_shapes=[
            buf(4, XL, TL, R), buf(XL, TL, RW), buf(*ttab.shape, dtype=BF16), buf(*xtab.shape, dtype=BF16),
            buf(2, TL, 2, XL, R), buf(8, TL, R), buf(TL, 8, R),
            buf(4, THETA, R), buf(4, X, R), buf(THETA, R), buf(3, X // 2, R),
            buf(4, THETA, R), buf(4, X, R), buf(THETA, R), buf(3, X // 2, R), buf(X, 2 * R),
            buf(4, XL, TL, R), buf(2, TL, 2, XL, R), buf(8, TL, R), buf(TL, 8, R),
            buf(4, XL, TL, R), buf(8, TL, R), buf(4, XL, TL, R), buf(XL, TL, RW),
            dma((4,)), dma((5,)),
            dma((2,)), dma((2,)), dma((2,)), dma((2,)), dma, dma, dma, dma,
            dma((2,)), dma((2,)), dma((2,)), dma((2,)), dma, dma, dma, dma,
        ],
        compiler_params=pltpu.CompilerParams(collective_id=0, has_side_effects=True),
    )(
        fields, wall_temp, fluid_metric.reshape(1, R), fluid_radial_inverses,
        wall_metric.reshape(1, RW), wall_inverse, ttab, xtab,
    )


def solution(mesh):
    in_specs = (
        P(None, ("ax", "grp"), "th", None),
        P(("ax", "grp"), "th", None),
        P(),
        P(),
        P(),
        P(),
    )
    out_specs = (P(None, ("ax", "grp"), "th", None), P(("ax", "grp"), "th", None))
    return jax.shard_map(shards, mesh=mesh, in_specs=in_specs, out_specs=out_specs, check_vma=False)
```

time: 182 us -> 65.9 us (0.36)
  local copies, waits for them, and re-layouts: 69.7 us -> 2.79 us
  Pallas kernels: 0 us -> 61.4 us
  waiting for transfers between devices: 34.4 us -> 0 us
  starting transfers between devices: 34.2 us -> 0 us
  other arithmetic: 26.7 us -> 0 us
  matrix products: 13 us -> 0 us
    pallas_call x0 -> x1, Pallas kernels: none -> 61.4 us  [shards(): pl.pallas_call(kernel, out_shape=(jax.ShapeDtypeStruct((4, XL, TL, R), F3...]
    all_to_all x4 -> x0, waiting for transfers between devices: 34.4 us -> none  [the longest x1 11.8 us: shards(): lax.all_to_all(lengthwise_bundle, ('ax', 'grp'), split_axis=1, concat_axi...]
    all_to_all x4 -> x0, starting transfers between devices: 34.2 us -> none  [the longest x1 13.6 us: shards(): lax.all_to_all(packed, 'th', split_axis=1, concat_axis=0, tiled=True)]
    transpose x8 -> x0, local copies, waits for them, and re-layouts: 24.8 us -> none  [the longest x2 6.42 us: shards(): lengthwise_bundle = jnp.concatenate([fields.reshape(comps, x_local, t_loc...]
    dot_general x4 -> x0, matrix products: 13 us -> none  [the longest x1 4.41 us: shards(): jnp.dot(circle_table, circle_in, precision=EXACT_PRECISION, preferred_ele...]
    slice x11 -> x0, local copies, waits for them, and re-layouts: 11.4 us -> none  [the longest x2 2.71 us: shards(): circle_home[:, :, :fluid_cols]]
    reshape x5 -> x0, local copies, waits for them, and re-layouts: 9.84 us -> none  [the longest x1 3.03 us: shards(): axial_terms = axial_home[:, :, :axial_cols].reshape(x_local, blocks, comp...]
    select_n x2 -> x0, other arithmetic: 9.1 us -> none  [tables(): jnp.where(nonzero, -parity * spacing * spacing / (2.0 * jnp.sin(polar_azi...]
  transfers between devices with their start and end apart: 4 -> 0, of which waited for: 4 -> 0; matrix products, arithmetic and copies ran while one was open for 40% -> 0% of each run, Pallas kernels for 0% -> 0%
where the time goes in v1:
time: 65.9 us; the launch traced here: 64.8 us
  Pallas kernels  61.4 us (93%)
  local copies, waits for them, and re-layouts  2.79 us (4%)
    pallas_call x1, Pallas kernels, shards(): pl.pallas_call(kernel, out_shape=(jax.ShapeDtypeStruct((4, XL, TL, R), F3...  61.4 us
    unnamed x4, local copies, waits for them, and re-layouts  2.79 us

profile of v1, /device:TPU:1, one launch (start us, length us, event | category | flops | bytes accessed | tf_op | source)
XLA Modules:
  0.0 64.8 jit_solution(196023393689882002)
XLA Ops:
  0.6 61.4 %shard_map.95 = (f32[4,16,24,128]{3,2,1,0:T(8,128)}, f32[16,24,64]{2,1,0:T(8,128)}) custom-call(f32[4,16,24,128]{3,2,1,0:T(8,128)} %fields_h.1, f32[16,24,64]{2,1,0:T(8,128)} %wall_h.1, f32[1,128]{1,0:T(1,128)} %bitcast.2, f32[2,128,128]{2,1,0:T(8,128)} %inv.1, f32[1,64]{1,0:T(1,128)} %bitcast.3, f32[64,64]{1,0:T(8,128)} %winv.1, ...), custom_call_target="tpu_custom_call" | custom-call | tf_op jit(solution)/shard_map/pallas_call | solution.py:475
  62.0 0.0 copy-start
  62.0 2.1 %copy.12 = f32[4,16,24,128]{3,2,1,0:T(8,128)} copy(f32[4,16,24,128]{3,2,1,0:T(8,128)} %get-tuple-element.4) | data formatting | bytes 1572864
  64.1 0.0 copy-done
  64.1 0.7 %copy.13 = f32[16,24,64]{2,1,0:T(8,128)} copy(f32[16,24,64]{2,1,0:T(8,128)S(1)} %copy-done) | data formatting | bytes 196608
Async XLA Ops:
  62.0 2.1 %copy-start = (f32[16,24,64]{2,1,0:T(8,128)S(1)}, f32[16,24,64]{2,1,0:T(8,128)}, u32[]{:S(2)}) copy-start(f32[16,24,64]{2,1,0:T(8,128)} %get-tuple-element.5) | copy-start | bytes 294916

commit v2 on v1

--- a/solution.py
+++ b/solution.py
@@ -68,6 +68,14 @@
     return lax.dot_general(a, b, (((1,), (1,)), ((), ())), preferred_element_type=F32)
 
 
+def apply_inverse(matrix, value):
+    m_high, m_low = split(matrix)
+    high, low = split(value)
+    return dot_t(
+        jnp.concatenate([high, low, high], axis=1), jnp.concatenate([m_high, m_high, m_low], axis=1)
+    )
+
+
 def apply_folded(table, rows, top, bottom):
     results = []
     for which, value in ((0, top + bottom), (1, top - bottom)):
@@ -79,15 +87,15 @@
 
 
 def kernel(
-    fields_h, wall_h, fm, inv, wm, winv, ttab_h, xtab_h,
-    out_h, wout_h,
-    F, W, ttab, xtab,
+    fields_h, wall_h, fm_h, inv_h, wm_h, winv_h, ttab_h, xtab_h,
+    done, rest, wdone,
+    F, W, fm, inv, wm, winv, ttab, xtab,
     fT, WP, wT,
     Qt, Qx, Wt, Wx,
     Rt, Rx, WRt, WRx, Wn,
     cih, axh, cwh, awh,
-    base, wbase, obuf, wobuf,
-    ld, st,
+    base, wbase,
+    ld,
     sT, rT, sX, rX, sWT, rWT, sWX, rWX,
     bsT, brT, bsX, brX, bsWT, brWT, bsWX, brWX,
 ):
@@ -121,14 +129,12 @@
     lax.fori_loop(1, NT, greet_t, 0)
     lax.fori_loop(1, NA, greet_a, 0)
 
-    load_f = pltpu.make_async_copy(fields_h, F, ld.at[0])
-    load_w = pltpu.make_async_copy(wall_h, W, ld.at[1])
-    load_t = pltpu.make_async_copy(ttab_h, ttab, ld.at[2])
-    load_x = pltpu.make_async_copy(xtab_h, xtab, ld.at[3])
-    load_f.start()
-    load_w.start()
-    load_t.start()
-    load_x.start()
+    sources = (fields_h, wall_h, fm_h, inv_h, wm_h, winv_h, ttab_h, xtab_h)
+    targets = (F, W, fm, inv, wm, winv, ttab, xtab)
+    loads = [pltpu.make_async_copy(src, dst, ld.at[i]) for i, (src, dst) in enumerate(zip(sources, targets))]
+    for load in loads:
+        load.start()
+    load_f, load_w, *load_rest = loads
     load_f.wait()
 
     F2 = F.reshape(4 * XL * TL, R)
@@ -206,6 +212,8 @@
     send_wall()
     send_chunk(1)
 
+    for load in load_rest:
+        load.wait()
     lane = lax.broadcasted_iota(jnp.int32, (TL, R), 1)
     m = fm[...]
     row_r = -0.5 * ADVECT_R * m
@@ -252,8 +260,6 @@
         return 0
 
     lax.fori_loop(0, 8, prepare, 0)
-    load_t.wait()
-    load_x.wait()
 
     def full(ref, sem):
         pltpu.make_async_copy(ref, ref, sem).wait()
@@ -382,32 +388,22 @@
 
     axh2 = axh.reshape(4 * XL * TL, R)
 
-    def inverse_parts(matrix):
-        high, low = split(matrix)
-        return jnp.concatenate([high, high, low], axis=1)
-
-    def value_parts(value):
-        high, low = split(value)
-        return jnp.concatenate([high, low, high], axis=1)
-
-    def finish(ch):
+    def gather(ch, out):
         full(cih.at[pl.ds(2 * ch, 2)], brT.at[ch])
         full(axh.at[ch], brX.at[ch])
-        for cc in range(2):
-            c = 2 * ch + cc
-
-            def gather(x, _):
+
+        def add(x, _):
+            for cc in range(2):
+                c = 2 * ch + cc
                 axial = axh2[pl.ds(ch * 2 * XL * TL + cc * XL + x, TL, stride=2 * XL), :]
-                base[c, x] = base[c, x] + cih[c, x] + axial
-                return 0
-
-            lax.fori_loop(0, XL, gather, 0)
-            matrix = inverse_parts(inv[1 if c == 3 else 0])
-            value = value_parts(base[c].reshape(XL * TL, R))
-            obuf[c] = dot_t(value, matrix).reshape(XL, TL, R)
-            pltpu.make_async_copy(obuf.at[c], out_h.at[c], st.at[c]).start()
-
-    finish(0)
+                out[cc, x] = base[c, x] + cih[c, x] + axial
+            return 0
+
+        lax.fori_loop(0, XL, add, 0)
+
+    gather(0, done)
+    for c in range(2):
+        done[c] = apply_inverse(inv[0], done[c].reshape(XL * TL, R)).reshape(XL, TL, R)
     full(cwh, brWT)
     full(awh, brWX)
     awh2 = awh.reshape(8 * TL, R)
@@ -417,14 +413,13 @@
         return 0
 
     lax.fori_loop(0, 8, gather_wall, 0)
-    value = value_parts(wbase[...].reshape(8 * TL, R))
+    value = wbase[...].reshape(8 * TL, R)
     nothing = jnp.zeros((RW, RW), F32)
     for h in range(2):
         pair = [winv[...], nothing] if h == 0 else [nothing, winv[...]]
-        matrix = inverse_parts(jnp.concatenate(pair, axis=1))
-        wobuf[8 * h:8 * h + 8] = dot_t(value, matrix).reshape(8, TL, RW)
-    pltpu.make_async_copy(wobuf, wout_h, st.at[4]).start()
-    finish(1)
+        matrix = jnp.concatenate(pair, axis=1)
+        wdone[8 * h:8 * h + 8] = apply_inverse(matrix, value).reshape(8, TL, RW)
+    gather(1, rest)
 
     for ch in range(2):
         full(F.at[pl.ds(0, 2), pl.ds(0, NT - 1)], sT.at[ch])
@@ -457,14 +452,26 @@
     def _():
         full(wT, sWX)
 
-    for c in range(4):
-        pltpu.make_async_copy(obuf.at[c], out_h.at[c], st.at[c]).wait()
-    pltpu.make_async_copy(wobuf, wout_h, st.at[4]).wait()
+
+def last_kernel(done, rest, wdone, inv, out_h, wout_h, buf, st):
+    copies = [
+        pltpu.make_async_copy(done, out_h.at[pl.ds(0, 2)], st.at[0]),
+        pltpu.make_async_copy(wdone, wout_h, st.at[1]),
+    ]
+    for copy in copies:
+        copy.start()
+    for c in range(2):
+        buf[c] = apply_inverse(inv[c], rest[c].reshape(XL * TL, R)).reshape(XL, TL, R)
+        copy = pltpu.make_async_copy(buf.at[c], out_h.at[2 + c], st.at[2 + c])
+        copy.start()
+        copies.append(copy)
+    for copy in copies:
+        copy.wait()
 
 
 def shards(fields, wall_temp, fluid_metric, fluid_radial_inverses, wall_metric, wall_inverse):
     vmem = pl.BlockSpec(memory_space=pltpu.VMEM)
-    hbm = pl.BlockSpec(memory_space=pl.ANY)
+    hbm = pl.BlockSpec(memory_space=pltpu.HBM)
     dma = pltpu.SemaphoreType.DMA
     ttab = jnp.asarray(folded_tables(THETA))
     xtab = jnp.asarray(folded_tables(X))
@@ -472,30 +479,41 @@
     def buf(*shape, dtype=F32):
         return pltpu.VMEM(shape, dtype)
 
+    done, rest, wdone = pl.pallas_call(
+        kernel,
+        out_shape=(buf(2, XL, TL, R), buf(2, XL, TL, R), buf(XL, TL, RW)),
+        in_specs=[hbm] * 8,
+        out_specs=(vmem, vmem, vmem),
+        scratch_shapes=[
+            buf(4, XL, TL, R), buf(XL, TL, RW), buf(1, R), buf(2, R, R), buf(1, RW), buf(RW, RW),
+            buf(*ttab.shape, dtype=BF16), buf(*xtab.shape, dtype=BF16),
+            buf(2, TL, 2, XL, R), buf(8, TL, R), buf(TL, 8, R),
+            buf(4, THETA, R), buf(4, X, R), buf(THETA, R), buf(3, X // 2, R),
+            buf(4, THETA, R), buf(4, X, R), buf(THETA, R), buf(3, X // 2, R), buf(X, 2 * R),
+            buf(4, XL, TL, R), buf(2, TL, 2, XL, R), buf(8, TL, R), buf(TL, 8, R),
+            buf(4, XL, TL, R), buf(8, TL, R),
+            dma((8,)),
+            dma((2,)), dma((2,)), dma((2,)), dma((2,)), dma, dma, dma, dma,
+            dma((2,)), dma((2,)), dma((2,)), dma((2,)), dma, dma, dma, dma,
+        ],
+        compiler_params=pltpu.CompilerParams(
+            collective_id=0, has_side_effects=True, vmem_limit_bytes=40 * 2**20
+        ),
+    )(
+        fields, wall_temp, fluid_metric.reshape(1, R), fluid_radial_inverses,
+        wall_metric.reshape(1, RW), wall_inverse, ttab, xtab,
+    )
     return pl.pallas_call(
-        kernel,
+        last_kernel,
         out_shape=(
             jax.ShapeDtypeStruct((4, XL, TL, R), F32),
             jax.ShapeDtypeStruct((XL, TL, RW), F32),
         ),
-        in_specs=[hbm, hbm, vmem, vmem, vmem, vmem, hbm, hbm],
+        in_specs=[vmem] * 4,
         out_specs=(hbm, hbm),
-        scratch_shapes=[
-            buf(4, XL, TL, R), buf(XL, TL, RW), buf(*ttab.shape, dtype=BF16), buf(*xtab.shape, dtype=BF16),
-            buf(2, TL, 2, XL, R), buf(8, TL, R), buf(TL, 8, R),
-            buf(4, THETA, R), buf(4, X, R), buf(THETA, R), buf(3, X // 2, R),
-            buf(4, THETA, R), buf(4, X, R), buf(THETA, R), buf(3, X // 2, R), buf(X, 2 * R),
-            buf(4, XL, TL, R), buf(2, TL, 2, XL, R), buf(8, TL, R), buf(TL, 8, R),
-            buf(4, XL, TL, R), buf(8, TL, R), buf(4, XL, TL, R), buf(XL, TL, RW),
-            dma((4,)), dma((5,)),
-            dma((2,)), dma((2,)), dma((2,)), dma((2,)), dma, dma, dma, dma,
-            dma((2,)), dma((2,)), dma((2,)), dma((2,)), dma, dma, dma, dma,
-        ],
-        compiler_params=pltpu.CompilerParams(collective_id=0, has_side_effects=True),
-    )(
-        fields, wall_temp, fluid_metric.reshape(1, R), fluid_radial_inverses,
-        wall_metric.reshape(1, RW), wall_inverse, ttab, xtab,
-    )
+        scratch_shapes=[buf(2, XL, TL, R), dma((4,))],
+        compiler_params=pltpu.CompilerParams(vmem_limit_bytes=16 * 2**20),
+    )(done, rest, wdone, fluid_radial_inverses)
 
 
 def solution(mesh):

time: 65.9 us -> 68.8 us (1.044)
  local copies, waits for them, and re-layouts: 2.79 us -> 6.73 us
  Pallas kernels: 61.4 us -> 60.3 us
    unnamed x4 -> x16, local copies, waits for them, and re-layouts: 2.79 us -> 6.73 us
    pallas_call x1 -> x2, Pallas kernels: 61.4 us -> 60.3 us  [the longest x1 59.3 us: shards(): pl.pallas_call(kernel, out_shape=(buf(2, XL, TL, R), buf(2, XL, TL, R), b...]
where the time goes in v2:
time: 68.8 us; the launch traced here: 67.7 us
  Pallas kernels  60.3 us (88%)
  local copies, waits for them, and re-layouts  6.73 us (10%)
    pallas_call x1, Pallas kernels, shards(): pl.pallas_call(kernel, out_shape=(buf(2, XL, TL, R), buf(2, XL, TL, R), b...  59.3 us
    unnamed x16, local copies, waits for them, and re-layouts  6.73 us

profile of v2, /device:TPU:1, one launch (start us, length us, event | category | flops | bytes accessed | tf_op | source)
XLA Modules:
  0.0 67.7 jit_solution(13563074976316953641)
XLA Ops:
  0.6 0.0 copy-start.6
  0.6 0.0 copy-start.7
  0.7 0.6 copy-done.6
  1.3 0.0 copy-done.7
  1.3 0.0 copy-start
  1.3 1.2 %copy-done = bf16[2,2,512,256]{3,2,1,0:T(8,128)(2,1)S(1)} copy-done((bf16[2,2,512,256]{3,2,1,0:T(8,128)(2,1)S(1)}, bf16[2,2,512,256]{3,2,1,0:T(8,128)(2,1)}, u32[]{:S(2)}) %copy-start) | copy-done | bytes 1048600
  2.5 0.0 copy-start.1
  2.5 1.1 %copy-done.1 = f32[4,16,24,128]{3,2,1,0:T(8,128)S(1)} copy-done((f32[4,16,24,128]{3,2,1,0:T(8,128)S(1)}, f32[4,16,24,128]{3,2,1,0:T(8,128)}, u32[]{:S(2)}) %copy-start.1) | copy-done | bytes 786456
  3.7 0.0 copy-start.2
  3.7 1.1 %copy-done.2 = bf16[2,2,384,192]{3,2,1,0:T(8,128)(2,1)S(1)} copy-done((bf16[2,2,384,192]{3,2,1,0:T(8,128)(2,1)S(1)}, bf16[2,2,384,192]{3,2,1,0:T(8,128)(2,1)}, u32[]{:S(2)}) %copy-start.2) | copy-done | bytes 589848
  4.8 0.0 copy-start.3
  4.8 0.9 %copy-done.3 = f32[2,128,128]{2,1,0:T(8,128)S(1)} copy-done((f32[2,128,128]{2,1,0:T(8,128)S(1)}, f32[2,128,128]{2,1,0:T(8,128)}, u32[]{:S(2)}) %copy-start.3) | copy-done | bytes 131096
  5.7 0.0 copy-start.4
  5.7 0.9 %copy-done.4 = f32[16,24,64]{2,1,0:T(8,128)S(1)} copy-done((f32[16,24,64]{2,1,0:T(8,128)S(1)}, f32[16,24,64]{2,1,0:T(8,128)}, u32[]{:S(2)}) %copy-start.4) | copy-done | bytes 98328
  6.6 0.0 copy-start.5
  6.6 0.8 %copy-done.5 = f32[64,64]{1,0:T(8,128)S(1)} copy-done((f32[64,64]{1,0:T(8,128)S(1)}, f32[64,64]{1,0:T(8,128)}, u32[]{:S(2)}) %copy-start.5) | copy-done | bytes 16408
  7.4 59.3 %shard_map.95 = (f32[2,16,24,128]{3,2,1,0:T(8,128)S(1)}, f32[2,16,24,128]{3,2,1,0:T(8,128)S(1)}, f32[16,24,64]{2,1,0:T(8,128)S(1)}) custom-call(f32[4,16,24,128]{3,2,1,0:T(8,128)S(1)} %copy-done.1, f32[16,24,64]{2,1,0:T(8,128)S(1)} %copy-done.4, f32[1,128]{1,0:T(1,128)S(1)} %bitcast.2, f32[2,128,128]{2,1,0:T(8,128)S(1)} %copy-done.3, f32[1,64]{1,0:T(1,128)S(1)} %bitcast.3, ...), custom_call_target="tpu_custom_call" | custom-call | tf_op jit(solution)/shard_map/pallas_call | solution.py:482
  66.7 1.0 %shard_map.96 = (f32[4,16,24,128]{3,2,1,0:T(8,128)}, f32[16,24,64]{2,1,0:T(8,128)}) custom-call(f32[2,16,24,128]{3,2,1,0:T(8,128)S(1)} %get-tuple-element.5.done, f32[2,16,24,128]{3,2,1,0:T(8,128)S(1)} %get-tuple-element.6.rest, f32[16,24,64]{2,1,0:T(8,128)S(1)} %get-tuple-element.7.wdone, f32[2,128,128]{2,1,0:T(8,128)S(1)} %copy-done.3), custom_call_target="tpu_custom_call" | custom-call | tf_op jit(solution)/shard_map/pallas_call | solution.py:506
Async XLA Ops:
  0.6 0.7 copy-start.6
  0.6 0.7 copy-start.7
  1.3 1.2 %copy-start = (bf16[2,2,512,256]{3,2,1,0:T(8,128)(2,1)S(1)}, bf16[2,2,512,256]{3,2,1,0:T(8,128)(2,1)}, u32[]{:S(2)}) copy-start(bf16[2,2,512,256]{3,2,1,0:T(8,128)(2,1)} %constant.5.clone.xtab_h) | copy-start | bytes 3145732
  2.5 1.1 %copy-start.1 = (f32[4,16,24,128]{3,2,1,0:T(8,128)S(1)}, f32[4,16,24,128]{3,2,1,0:T(8,128)}, u32[]{:S(2)}) copy-start(f32[4,16,24,128]{3,2,1,0:T(8,128)} %fields_h.1) | copy-start | bytes 2359300
  3.7 1.1 %copy-start.2 = (bf16[2,2,384,192]{3,2,1,0:T(8,128)(2,1)S(1)}, bf16[2,2,384,192]{3,2,1,0:T(8,128)(2,1)}, u32[]{:S(2)}) copy-start(bf16[2,2,384,192]{3,2,1,0:T(8,128)(2,1)} %constant.4.clone.ttab_h) | copy-start | bytes 1769476
  4.8 0.9 %copy-start.3 = (f32[2,128,128]{2,1,0:T(8,128)S(1)}, f32[2,128,128]{2,1,0:T(8,128)}, u32[]{:S(2)}) copy-start(f32[2,128,128]{2,1,0:T(8,128)} %inv.1) | copy-start | bytes 393220
  5.7 0.9 %copy-start.4 = (f32[16,24,64]{2,1,0:T(8,128)S(1)}, f32[16,24,64]{2,1,0:T(8,128)}, u32[]{:S(2)}) copy-start(f32[16,24,64]{2,1,0:T(8,128)} %wall_h.1) | copy-start | bytes 294916
  6.6 0.8 %copy-start.5 = (f32[64,64]{1,0:T(8,128)S(1)}, f32[64,64]{1,0:T(8,128)}, u32[]{:S(2)}) copy-start(f32[64,64]{1,0:T(8,128)} %winv_h.1) | copy-start | bytes 49156

commit v3 on v2

--- a/solution.py
+++ b/solution.py
@@ -68,12 +68,14 @@
     return lax.dot_general(a, b, (((1,), (1,)), ((), ())), preferred_element_type=F32)
 
 
-def apply_inverse(matrix, value):
-    m_high, m_low = split(matrix)
+def inverse_parts(matrix):
+    high, low = split(matrix)
+    return jnp.concatenate([high, high, low], axis=1)
+
+
+def apply_inverse(parts, value):
     high, low = split(value)
-    return dot_t(
-        jnp.concatenate([high, low, high], axis=1), jnp.concatenate([m_high, m_high, m_low], axis=1)
-    )
+    return dot_t(jnp.concatenate([high, low, high], axis=1), parts)
 
 
 def apply_folded(table, rows, top, bottom):
@@ -88,7 +90,7 @@
 
 def kernel(
     fields_h, wall_h, fm_h, inv_h, wm_h, winv_h, ttab_h, xtab_h,
-    done, rest, wdone,
+    done, rest, wdone, parts,
     F, W, fm, inv, wm, winv, ttab, xtab,
     fT, WP, wT,
     Qt, Qx, Wt, Wx,
@@ -260,6 +262,8 @@
         return 0
 
     lax.fori_loop(0, 8, prepare, 0)
+    for i in range(2):
+        parts[i] = inverse_parts(inv[i])
 
     def full(ref, sem):
         pltpu.make_async_copy(ref, ref, sem).wait()
@@ -403,7 +407,7 @@
 
     gather(0, done)
     for c in range(2):
-        done[c] = apply_inverse(inv[0], done[c].reshape(XL * TL, R)).reshape(XL, TL, R)
+        done[c] = apply_inverse(parts[0], done[c].reshape(XL * TL, R)).reshape(XL, TL, R)
     full(cwh, brWT)
     full(awh, brWX)
     awh2 = awh.reshape(8 * TL, R)
@@ -417,7 +421,7 @@
     nothing = jnp.zeros((RW, RW), F32)
     for h in range(2):
         pair = [winv[...], nothing] if h == 0 else [nothing, winv[...]]
-        matrix = jnp.concatenate(pair, axis=1)
+        matrix = inverse_parts(jnp.concatenate(pair, axis=1))
         wdone[8 * h:8 * h + 8] = apply_inverse(matrix, value).reshape(8, TL, RW)
     gather(1, rest)
 
@@ -453,7 +457,7 @@
         full(wT, sWX)
 
 
-def last_kernel(done, rest, wdone, inv, out_h, wout_h, buf, st):
+def last_kernel(done, rest, wdone, parts, out_h, wout_h, buf, st):
     copies = [
         pltpu.make_async_copy(done, out_h.at[pl.ds(0, 2)], st.at[0]),
         pltpu.make_async_copy(wdone, wout_h, st.at[1]),
@@ -461,7 +465,7 @@
     for copy in copies:
         copy.start()
     for c in range(2):
-        buf[c] = apply_inverse(inv[c], rest[c].reshape(XL * TL, R)).reshape(XL, TL, R)
+        buf[c] = apply_inverse(parts[c], rest[c].reshape(XL * TL, R)).reshape(XL, TL, R)
         copy = pltpu.make_async_copy(buf.at[c], out_h.at[2 + c], st.at[2 + c])
         copy.start()
         copies.append(copy)
@@ -479,11 +483,11 @@
     def buf(*shape, dtype=F32):
         return pltpu.VMEM(shape, dtype)
 
-    done, rest, wdone = pl.pallas_call(
+    done, rest, wdone, parts = pl.pallas_call(
         kernel,
-        out_shape=(buf(2, XL, TL, R), buf(2, XL, TL, R), buf(XL, TL, RW)),
+        out_shape=(buf(2, XL, TL, R), buf(2, XL, TL, R), buf(XL, TL, RW), buf(2, R, 3 * R, dtype=BF16)),
         in_specs=[hbm] * 8,
-        out_specs=(vmem, vmem, vmem),
+        out_specs=(vmem,) * 4,
         scratch_shapes=[
             buf(4, XL, TL, R), buf(XL, TL, RW), buf(1, R), buf(2, R, R), buf(1, RW), buf(RW, RW),
             buf(*ttab.shape, dtype=BF16), buf(*xtab.shape, dtype=BF16),
@@ -497,7 +501,7 @@
             dma((2,)), dma((2,)), dma((2,)), dma((2,)), dma, dma, dma, dma,
         ],
         compiler_params=pltpu.CompilerParams(
-            collective_id=0, has_side_effects=True, vmem_limit_bytes=40 * 2**20
+            collective_id=0, has_side_effects=True, vmem_limit_bytes=64128 * 2**10
         ),
     )(
         fields, wall_temp, fluid_metric.reshape(1, R), fluid_radial_inverses,
@@ -513,7 +517,7 @@
         out_specs=(hbm, hbm),
         scratch_shapes=[buf(2, XL, TL, R), dma((4,))],
         compiler_params=pltpu.CompilerParams(vmem_limit_bytes=16 * 2**20),
-    )(done, rest, wdone, fluid_radial_inverses)
+    )(done, rest, wdone, parts)
 
 
 def solution(mesh):

time: 68.8 us -> 62.4 us (0.907)
  the two profiles are of different devices: /device:TPU:1 before, /device:TPU:91 now
where the time goes in v3:
time: 62.4 us; the launch traced here: 62.3 us
  Pallas kernels  61.6 us (99%)
  between operations  0.64 us (1%)
    pallas_call x1, Pallas kernels, shards(): pl.pallas_call(kernel, out_shape=(buf(2, XL, TL, R), buf(2, XL, TL, R), b...  60.6 us

profile of v3, /device:TPU:91, one launch (start us, length us, event | category | flops | bytes accessed | tf_op | source)
XLA Modules:
  0.0 62.3 jit_solution(3717682303005446524)
XLA Ops:
  0.6 60.6 %shard_map.95 = (f32[2,16,24,128]{3,2,1,0:T(8,128)S(1)}, f32[2,16,24,128]{3,2,1,0:T(8,128)S(1)}, f32[16,24,64]{2,1,0:T(8,128)S(1)}, bf16[2,128,384]{2,1,0:T(8,128)(2,1)S(1)}) custom-call(f32[4,16,24,128]{3,2,1,0:T(8,128)} %fields_h.1, f32[16,24,64]{2,1,0:T(8,128)} %wall_h.1, f32[1,128]{1,0:T(1,128)} %bitcast.2, f32[2,128,128]{2,1,0:T(8,128)} %inv_h.1, ...), custom_call_target="tpu_custom_call" | custom-call | tf_op jit(solution)/shard_map/pallas_call | solution.py:486
  61.2 1.0 %shard_map.96 = (f32[4,16,24,128]{3,2,1,0:T(8,128)}, f32[16,24,64]{2,1,0:T(8,128)}) custom-call(f32[2,16,24,128]{3,2,1,0:T(8,128)S(1)} %get-tuple-element.6.done, f32[2,16,24,128]{3,2,1,0:T(8,128)S(1)} %get-tuple-element.7.rest, f32[16,24,64]{2,1,0:T(8,128)S(1)} %get-tuple-element.8.wdone, bf16[2,128,384]{2,1,0:T(8,128)(2,1)S(1)} %get-tuple-element.9.parts), custom_call_target="tpu_custom_call" | custom-call | tf_op jit(solution)/shard_map/pallas_call | solution.py:510

commit v4 on v3

--- a/solution.py
+++ b/solution.py
@@ -109,27 +109,22 @@
     core = lax.rem(ax, 2)
     xh = lax.div(th, 8)
     z = lax.rem(th, 8)
-    odd_y = lax.rem(y, 2)
-    x_wall = jnp.logical_and(core == 0, grp == odd_y)
-    x_fluid = jnp.logical_not(x_wall)
-    my_theta = 3 * y + core * (1 + grp)
+    x_whole = core == 0
+    x_half = core == 1
+    my_theta = 3 * y + 2 * grp
     t_wall = xh == lax.rem(z, 2)
 
     barrier = pltpu.get_barrier_semaphore()
 
-    def greet_t(k, _):
-        pl.semaphore_signal(barrier, inc=1, device_id=(ax, lax.rem(th + k, NT), grp), device_id_type=MESH)
-        return 0
-
-    def greet_a(k, _):
-        peer = lax.rem(a + k, NA)
-        pl.semaphore_signal(
-            barrier, inc=1, device_id=(lax.div(peer, 2), th, lax.rem(peer, 2)), device_id_type=MESH
-        )
-        return 0
-
-    lax.fori_loop(1, NT, greet_t, 0)
-    lax.fori_loop(1, NA, greet_a, 0)
+    for far in (4, 3, 5, 2, 6, 1, 7, 0):
+        for flip in (1, 0):
+            if far or flip:
+                peer = lax.rem(xh + flip, 2) * 8 + lax.rem(z + far, 8)
+                pl.semaphore_signal(barrier, inc=1, device_id=(ax, peer, grp), device_id_type=MESH)
+        for flip in range(4):
+            if far or flip:
+                peer = (2 * lax.rem(y + far, 8) + lax.rem(core + flip // 2, 2), th, lax.rem(grp + flip, 2))
+                pl.semaphore_signal(barrier, inc=1, device_id=peer, device_id_type=MESH)
 
     sources = (fields_h, wall_h, fm_h, inv_h, wm_h, winv_h, ttab_h, xtab_h)
     targets = (F, W, fm, inv, wm, winv, ttab, xtab)
@@ -143,10 +138,27 @@
 
     def turn(t, _):
         for c in range(4):
-            fT[c // 2, t, c % 2] = F2[pl.ds(c * XL * TL + t, XL, stride=TL), :]
+            fT[c // 2, 2 * t + c % 2] = F2[pl.ds(c * XL * TL + t, XL, stride=TL), :]
         return 0
 
     lax.fori_loop(0, TL, turn, 0)
+    low = lax.broadcasted_iota(jnp.int32, (XL, R), 1) < RW
+
+    def swap_halves(ref, ch, yy):
+        at = 6 * yy + 2
+        one, two = ref[ch, at], ref[ch, at + 1]
+        ref[ch, at] = jnp.where(low, one, pltpu.roll(two, RW, axis=1))
+        ref[ch, at + 1] = jnp.where(low, pltpu.roll(one, RW, axis=1), two)
+
+    def swap_all(ref, ch):
+        def step(yy, _):
+            swap_halves(ref, ch, yy)
+            return 0
+
+        lax.fori_loop(0, 8, step, 0)
+
+    swap_all(fT, 0)
+    swap_all(fT, 1)
     load_w.wait()
     for p in range(8):
         WP[p] = jnp.concatenate([W[p], W[p + 8]], axis=1)
@@ -182,14 +194,15 @@
                     sT.at[ch], rT.at[ch], (ax, t, grp),
                 )
             yy = lax.rem(y + offset(i), 8)
-            for k in range(3):
-                theta = 3 * yy + k
-                c_to = (k + 1) // 2
-                g_to = k // 2 + (1 - c_to) * (1 - lax.rem(yy, 2))
-                a_to = 4 * yy + 2 * c_to + g_to
-                send(
-                    a_to != a, fT.at[ch, theta], Qx.at[pl.ds(2 * ch, 2), pl.ds(XL * a, XL)],
-                    sX.at[ch], rX.at[ch], (2 * yy + c_to, th, g_to),
+            for g_to in range(2):
+                a_to = 4 * yy + g_to
+                send(
+                    a_to != a, fT.at[ch, pl.ds(6 * yy + 4 * g_to, 2)], Qx.at[pl.ds(2 * ch, 2), pl.ds(XL * a, XL)],
+                    sX.at[ch], rX.at[ch], (2 * yy, th, g_to),
+                )
+                send(
+                    a_to + 2 != a, fT.at[ch, 6 * yy + 2 + g_to], Qx.at[ch, pl.ds(XL * a, XL)],
+                    sX.at[ch], rX.at[ch], (2 * yy + 1, th, g_to),
                 )
             return 0
 
@@ -201,11 +214,12 @@
             t = lax.rem(p, 2) * 8 + p
             send(t != th, WP.at[p], Wt.at[pl.ds(TL * th, TL)], sWT, rWT, (ax, t, grp))
             yy = lax.rem(y + offset(i), 8)
-            a_to = 4 * yy + lax.rem(yy, 2)
-            send(
-                a_to != a, wT.at[pl.ds(3 * yy, 3)], Wx.at[:, pl.ds(8 * a, 8)],
-                sWX, rWX, (2 * yy, th, lax.rem(yy, 2)),
-            )
+            for g_to in range(2):
+                slots = pl.ds(0, 2 - g_to)
+                send(
+                    4 * yy + 2 + g_to != a, wT.at[pl.ds(3 * yy + 2 * g_to, 2 - g_to)], Wx.at[slots, pl.ds(8 * a, 8)],
+                    sWX, rWX, (2 * yy + 1, th, g_to),
+                )
             return 0
 
         lax.fori_loop(0, 8, step, 0)
@@ -317,7 +331,33 @@
             for k in range(4):
                 a_to = 4 * yy + k
                 send(
-                    a_to != a, Rx.at[both, pl.ds(XL * a_to, XL)], axh.at[ch, my_theta],
+                    a_to != a, Rx.at[both, pl.ds(XL * a_to, XL)], axh.at[ch, pl.ds(2 * my_theta, 2)],
+                    bsX.at[ch], brX.at[ch], (2 * yy + k // 2, th, k % 2),
+                )
+            return 0
+
+        lax.fori_loop(0, 8, step, 0)
+
+    lam_halves = jnp.where(lane[:1] < RW, LATERAL_U, LATERAL_T)
+
+    def axial_half(ch):
+        full(Qx.at[ch], rX.at[ch])
+        firsts = apply_folded(xtab, slice(0, half_x), Qx[ch, :half_x], Qx[ch, half_x:])
+        seconds = apply_folded(xtab, slice(half_x, X), Qx[ch, :half_x], Qx[ch, half_x:])
+        lam_row = jnp.where(ch == 1, lam_halves, LATERAL_U)
+        low_x = lax.broadcasted_iota(jnp.int32, (half_x, R), 1) < RW
+        for h in range(2):
+            rows = slice(h * half_x, (h + 1) * half_x)
+            stream = Qx[0, rows] * (-ADVECT_X)
+            stream = jnp.where(low_x, stream, pltpu.roll(stream, RW, axis=1))
+            Rx[ch, rows] = stream * firsts[h] + seconds[h] * lam_row
+
+        def step(i, _):
+            yy = lax.rem(y + offset(i), 8)
+            for k in range(4):
+                a_to = 4 * yy + k
+                send(
+                    a_to != a, Rx.at[ch, pl.ds(XL * a_to, XL)], axh.at[ch, 6 * y + 2 + grp],
                     bsX.at[ch], brX.at[ch], (2 * yy + k // 2, th, k % 2),
                 )
             return 0
@@ -340,18 +380,18 @@
 
     low8 = lax.broadcasted_iota(jnp.int32, (8, R), 1) < RW
 
-    def axial_wall():
-        full(Wx, rWX)
+    def axial_wall(g):
+        slots = pl.ds(0, 2 - g)
+        full(Wx.at[slots], rWX)
 
         def unpack(s, _):
             rows = pl.ds(pl.multiple_of(8 * s, 8), 8)
-            w0, w1, w2 = Wx[0, rows], Wx[1, rows], Wx[2, rows]
             even = pl.ds(pl.multiple_of(16 * s, 8), 8)
             odd = pl.ds(pl.multiple_of(16 * s + 8, 8), 8)
-            Wn[even, 0:R] = jnp.where(low8, w0, pltpu.roll(w1, RW, axis=1))
-            Wn[odd, 0:R] = jnp.where(low8, pltpu.roll(w0, RW, axis=1), w1)
-            Wn[even, R:2 * R] = w2
-            Wn[odd, R:2 * R] = pltpu.roll(w2, RW, axis=1)
+            w0 = Wx[0, rows]
+            w1 = Wx[1 - g, rows]
+            Wn[even] = jnp.where(low8, w0, pltpu.roll(w1, RW, axis=1))
+            Wn[odd] = jnp.where(low8, pltpu.roll(w0, RW, axis=1), w1)
             return 0
 
         lax.fori_loop(0, NA, unpack, 0)
@@ -361,12 +401,11 @@
 
         def pack(s, _):
             rows = pl.ds(pl.multiple_of(8 * s, 8), 8)
-            even = pl.ds(pl.multiple_of(16 * s, 8), 8)
-            odd = pl.ds(pl.multiple_of(16 * s + 8, 8), 8)
-            e01, o01 = Wn[even, 0:R], Wn[odd, 0:R]
-            WRx[0, rows] = jnp.where(low8, e01, pltpu.roll(o01, RW, axis=1))
-            WRx[1, rows] = jnp.where(low8, pltpu.roll(e01, RW, axis=1), o01)
-            WRx[2, rows] = jnp.where(low8, Wn[even, R:2 * R], pltpu.roll(Wn[odd, R:2 * R], RW, axis=1))
+            even = Wn[pl.ds(pl.multiple_of(16 * s, 8), 8)]
+            odd = Wn[pl.ds(pl.multiple_of(16 * s + 8, 8), 8)]
+            WRx[0, rows] = jnp.where(low8, even, pltpu.roll(odd, RW, axis=1))
+            if g == 0:
+                WRx[1, rows] = jnp.where(low8, pltpu.roll(even, RW, axis=1), odd)
             return 0
 
         lax.fori_loop(0, NA, pack, 0)
@@ -376,7 +415,7 @@
             for k in range(4):
                 a_to = 4 * yy + k
                 send(
-                    a_to != a, WRx.at[:, pl.ds(8 * a_to, 8)], awh.at[pl.ds(3 * y, 3)],
+                    a_to != a, WRx.at[slots, pl.ds(8 * a_to, 8)], awh.at[pl.ds(3 * y + 2 * g, 2 - g)],
                     bsWX, brWX, (2 * yy + k // 2, th, k % 2),
                 )
             return 0
@@ -384,17 +423,21 @@
         lax.fori_loop(0, 8, step, 0)
 
     theta_chunk(0)
-    pl.when(x_fluid)(lambda: axial_chunk(0))
-    pl.when(x_wall)(axial_wall)
+    pl.when(x_whole)(lambda: axial_chunk(0))
+    pl.when(x_half)(lambda: axial_half(0))
+    pl.when(jnp.logical_and(x_half, grp == 0))(lambda: axial_wall(0))
+    pl.when(jnp.logical_and(x_half, grp == 1))(lambda: axial_wall(1))
     pl.when(t_wall)(theta_wall)
     theta_chunk(1)
-    pl.when(x_fluid)(lambda: axial_chunk(1))
+    pl.when(x_whole)(lambda: axial_chunk(1))
+    pl.when(x_half)(lambda: axial_half(1))
 
     axh2 = axh.reshape(4 * XL * TL, R)
 
     def gather(ch, out):
         full(cih.at[pl.ds(2 * ch, 2)], brT.at[ch])
         full(axh.at[ch], brX.at[ch])
+        swap_all(axh, ch)
 
         def add(x, _):
             for cc in range(2):
@@ -429,14 +472,15 @@
         full(F.at[pl.ds(0, 2), pl.ds(0, NT - 1)], sT.at[ch])
         full(F.at[pl.ds(0, 2), pl.ds(0, NT - 1)], bsT.at[ch])
 
-        @pl.when(x_fluid)
+        @pl.when(x_whole)
         def _():
-            full(fT.at[ch, pl.ds(0, TL - 1)], sX.at[ch])
+            full(fT.at[ch, pl.ds(0, 2 * TL - 2)], sX.at[ch])
             full(Rx.at[pl.ds(0, 2), pl.ds(0, X - XL)], bsX.at[ch])
 
-        @pl.when(x_wall)
+        @pl.when(x_half)
         def _():
-            full(fT.at[ch], sX.at[ch])
+            full(fT.at[ch, pl.ds(0, 2 * TL - 1)], sX.at[ch])
+            full(Rx.at[0, pl.ds(0, X - XL)], bsX.at[ch])
 
     @pl.when(t_wall)
     def _():
@@ -447,14 +491,15 @@
     def _():
         full(WP, sWT)
 
-    @pl.when(x_wall)
-    def _():
-        full(wT.at[pl.ds(0, TL - 3)], sWX)
-        full(WRx.at[:, pl.ds(0, 8 * (NA - 1))], bsWX)
-
-    @pl.when(x_fluid)
+    @pl.when(x_whole)
     def _():
         full(wT, sWX)
+
+    for g in range(2):
+        @pl.when(jnp.logical_and(x_half, grp == g))
+        def _():
+            full(wT.at[pl.ds(0, TL - 2 + g)], sWX)
+            full(WRx.at[pl.ds(0, 2 - g), pl.ds(0, 8 * (NA - 1))], bsWX)
 
 
 def last_kernel(done, rest, wdone, parts, out_h, wout_h, buf, st):
@@ -491,10 +536,10 @@
         scratch_shapes=[
             buf(4, XL, TL, R), buf(XL, TL, RW), buf(1, R), buf(2, R, R), buf(1, RW), buf(RW, RW),
             buf(*ttab.shape, dtype=BF16), buf(*xtab.shape, dtype=BF16),
-            buf(2, TL, 2, XL, R), buf(8, TL, R), buf(TL, 8, R),
-            buf(4, THETA, R), buf(4, X, R), buf(THETA, R), buf(3, X // 2, R),
-            buf(4, THETA, R), buf(4, X, R), buf(THETA, R), buf(3, X // 2, R), buf(X, 2 * R),
-            buf(4, XL, TL, R), buf(2, TL, 2, XL, R), buf(8, TL, R), buf(TL, 8, R),
+            buf(2, 2 * TL, XL, R), buf(8, TL, R), buf(TL, 8, R),
+            buf(4, THETA, R), buf(4, X, R), buf(THETA, R), buf(2, X // 2, R),
+            buf(4, THETA, R), buf(4, X, R), buf(THETA, R), buf(2, X // 2, R), buf(X, R),
+            buf(4, XL, TL, R), buf(2, 2 * TL, XL, R), buf(8, TL, R), buf(TL, 8, R),
             buf(4, XL, TL, R), buf(8, TL, R),
             dma((8,)),
             dma((2,)), dma((2,)), dma((2,)), dma((2,)), dma, dma, dma, dma,

time: 62.4 us -> 61.2 us (0.981)
  the two profiles are of different devices: /device:TPU:91 before, /device:TPU:1 now
where the time goes in v4:
time: 61.2 us; the launch traced here: 61 us
  Pallas kernels  60.4 us (99%)
  between operations  0.64 us (1%)
    pallas_call x1, Pallas kernels, shards(): pl.pallas_call(kernel, out_shape=(buf(2, XL, TL, R), buf(2, XL, TL, R), b...  59.3 us

profile of v4, /device:TPU:1, one launch (start us, length us, event | category | flops | bytes accessed | tf_op | source)
XLA Modules:
  0.0 61.0 jit_solution(10905825498075556599)
XLA Ops:
  0.6 59.3 %shard_map.95 = (f32[2,16,24,128]{3,2,1,0:T(8,128)S(1)}, f32[2,16,24,128]{3,2,1,0:T(8,128)S(1)}, f32[16,24,64]{2,1,0:T(8,128)S(1)}, bf16[2,128,384]{2,1,0:T(8,128)(2,1)S(1)}) custom-call(f32[4,16,24,128]{3,2,1,0:T(8,128)} %fields_h.1, f32[16,24,64]{2,1,0:T(8,128)} %wall_h.1, f32[1,128]{1,0:T(1,128)} %bitcast.2, f32[2,128,128]{2,1,0:T(8,128)} %inv_h.1, ...), custom_call_target="tpu_custom_call" | custom-call | tf_op jit(solution)/shard_map/pallas_call | solution.py:531
  60.0 1.0 %shard_map.96 = (f32[4,16,24,128]{3,2,1,0:T(8,128)}, f32[16,24,64]{2,1,0:T(8,128)}) custom-call(f32[2,16,24,128]{3,2,1,0:T(8,128)S(1)} %get-tuple-element.6.done, f32[2,16,24,128]{3,2,1,0:T(8,128)S(1)} %get-tuple-element.7.rest, f32[16,24,64]{2,1,0:T(8,128)S(1)} %get-tuple-element.8.wdone, bf16[2,128,384]{2,1,0:T(8,128)(2,1)S(1)} %get-tuple-element.9.parts), custom_call_target="tpu_custom_call" | custom-call | tf_op jit(solution)/shard_map/pallas_call | solution.py:555

commit v5 on v4

--- a/solution.py
+++ b/solution.py
@@ -126,22 +126,26 @@
                 peer = (2 * lax.rem(y + far, 8) + lax.rem(core + flip // 2, 2), th, lax.rem(grp + flip, 2))
                 pl.semaphore_signal(barrier, inc=1, device_id=peer, device_id_type=MESH)
 
-    sources = (fields_h, wall_h, fm_h, inv_h, wm_h, winv_h, ttab_h, xtab_h)
-    targets = (F, W, fm, inv, wm, winv, ttab, xtab)
+    halves = [ref.at[pl.ds(2 * ch, 2)] for ref in (fields_h, F) for ch in range(2)]
+    sources = (*halves[:2], wall_h, fm_h, inv_h, wm_h, winv_h, ttab_h, xtab_h)
+    targets = (*halves[2:], W, fm, inv, wm, winv, ttab, xtab)
     loads = [pltpu.make_async_copy(src, dst, ld.at[i]) for i, (src, dst) in enumerate(zip(sources, targets))]
     for load in loads:
         load.start()
-    load_f, load_w, *load_rest = loads
-    load_f.wait()
+    *load_f, load_w = loads[:3]
+    load_rest = loads[3:]
 
     F2 = F.reshape(4 * XL * TL, R)
 
-    def turn(t, _):
-        for c in range(4):
-            fT[c // 2, 2 * t + c % 2] = F2[pl.ds(c * XL * TL + t, XL, stride=TL), :]
-        return 0
-
-    lax.fori_loop(0, TL, turn, 0)
+    def turn(ch):
+        def step(t, _):
+            for cc in range(2):
+                fT[ch, 2 * t + cc] = F2[pl.ds((2 * ch + cc) * XL * TL + t, XL, stride=TL), :]
+            return 0
+
+        lax.fori_loop(0, TL, step, 0)
+        swap_all(fT, ch)
+
     low = lax.broadcasted_iota(jnp.int32, (XL, R), 1) < RW
 
     def swap_halves(ref, ch, yy):
@@ -157,16 +161,13 @@
 
         lax.fori_loop(0, 8, step, 0)
 
-    swap_all(fT, 0)
-    swap_all(fT, 1)
-    load_w.wait()
-    for p in range(8):
-        WP[p] = jnp.concatenate([W[p], W[p + 8]], axis=1)
-    WP2 = WP.reshape(8 * TL, R)
-    for t in range(TL):
-        wT[t] = WP2[pl.ds(t, 8, stride=TL), :]
-
-    pl.semaphore_wait(barrier, NT - 1 + NA - 1)
+    def pair_walls():
+        load_w.wait()
+        for p in range(8):
+            WP[p] = jnp.concatenate([W[p], W[p + 8]], axis=1)
+        WP2 = WP.reshape(8 * TL, R)
+        for t in range(TL):
+            wT[t] = WP2[pl.ds(t, 8, stride=TL), :]
 
     def offset(i):
         return 4 + lax.div(i + 1, 2) * (1 - 2 * lax.rem(i, 2))
@@ -186,13 +187,23 @@
         return lax.rem(xh + flip, 2) * 8 + lax.rem(z + offset(i), 8)
 
     def send_chunk(ch):
-        def step(i, _):
+        load_f[ch].wait()
+        if ch == 0:
+            pl.semaphore_wait(barrier, NT - 1 + NA - 1)
+
+        def step_t(i, _):
             for flip in (1, 0):
                 t = theta_peer(i, flip)
                 send(
                     t != th, F.at[pl.ds(2 * ch, 2), t], Qt.at[pl.ds(2 * ch, 2), pl.ds(TL * th, TL)],
                     sT.at[ch], rT.at[ch], (ax, t, grp),
                 )
+            return 0
+
+        lax.fori_loop(0, 8, step_t, 0)
+        turn(ch)
+
+        def step(i, _):
             yy = lax.rem(y + offset(i), 8)
             for g_to in range(2):
                 a_to = 4 * yy + g_to
@@ -225,6 +236,7 @@
         lax.fori_loop(0, 8, step, 0)
 
     send_chunk(0)
+    pair_walls()
     send_wall()
     send_chunk(1)
 
@@ -541,7 +553,7 @@
             buf(4, THETA, R), buf(4, X, R), buf(THETA, R), buf(2, X // 2, R), buf(X, R),
             buf(4, XL, TL, R), buf(2, 2 * TL, XL, R), buf(8, TL, R), buf(TL, 8, R),
             buf(4, XL, TL, R), buf(8, TL, R),
-            dma((8,)),
+            dma((9,)),
             dma((2,)), dma((2,)), dma((2,)), dma((2,)), dma, dma, dma, dma,
             dma((2,)), dma((2,)), dma((2,)), dma((2,)), dma, dma, dma, dma,
         ],

time: 61.2 us -> 61.2 us (level)
  no operation moved by 1% of the time
where the time goes in v5:
time: 61.2 us; the launch traced here: 61 us
  Pallas kernels  60.4 us (99%)
  between operations  0.64 us (1%)
    pallas_call x1, Pallas kernels, shards(): pl.pallas_call(kernel, out_shape=(buf(2, XL, TL, R), buf(2, XL, TL, R), b...  59.3 us

profile of v5, /device:TPU:1, one launch (start us, length us, event | category | flops | bytes accessed | tf_op | source)
XLA Modules:
  0.0 61.0 jit_solution(15741963879838397767)
XLA Ops:
  0.6 59.3 %shard_map.95 = (f32[2,16,24,128]{3,2,1,0:T(8,128)S(1)}, f32[2,16,24,128]{3,2,1,0:T(8,128)S(1)}, f32[16,24,64]{2,1,0:T(8,128)S(1)}, bf16[2,128,384]{2,1,0:T(8,128)(2,1)S(1)}) custom-call(f32[4,16,24,128]{3,2,1,0:T(8,128)} %fields_h.1, f32[16,24,64]{2,1,0:T(8,128)} %wall_h.1, f32[1,128]{1,0:T(1,128)} %bitcast.2, f32[2,128,128]{2,1,0:T(8,128)} %inv_h.1, ...), custom_call_target="tpu_custom_call" | custom-call | tf_op jit(solution)/shard_map/pallas_call | solution.py:543
  60.0 1.1 %shard_map.96 = (f32[4,16,24,128]{3,2,1,0:T(8,128)}, f32[16,24,64]{2,1,0:T(8,128)}) custom-call(f32[2,16,24,128]{3,2,1,0:T(8,128)S(1)} %get-tuple-element.6.done, f32[2,16,24,128]{3,2,1,0:T(8,128)S(1)} %get-tuple-element.7.rest, f32[16,24,64]{2,1,0:T(8,128)S(1)} %get-tuple-element.8.wdone, bf16[2,128,384]{2,1,0:T(8,128)(2,1)S(1)} %get-tuple-element.9.parts), custom_call_target="tpu_custom_call" | custom-call | tf_op jit(solution)/shard_map/pallas_call | solution.py:567

commit v6 on v5

--- a/solution.py
+++ b/solution.py
@@ -138,12 +138,14 @@
     F2 = F.reshape(4 * XL * TL, R)
 
     def turn(ch):
-        def step(t, _):
-            for cc in range(2):
-                fT[ch, 2 * t + cc] = F2[pl.ds((2 * ch + cc) * XL * TL + t, XL, stride=TL), :]
-            return 0
-
-        lax.fori_loop(0, TL, step, 0)
+        def step(group, _):
+            for i in range(4):
+                t = 4 * group + i
+                for cc in range(2):
+                    fT[ch, 2 * t + cc] = F2[pl.ds((2 * ch + cc) * XL * TL + t, XL, stride=TL), :]
+            return 0
+
+        lax.fori_loop(0, TL // 4, step, 0)
         swap_all(fT, ch)
 
     low = lax.broadcasted_iota(jnp.int32, (XL, R), 1) < RW
@@ -155,11 +157,12 @@
         ref[ch, at + 1] = jnp.where(low, pltpu.roll(one, RW, axis=1), two)
 
     def swap_all(ref, ch):
-        def step(yy, _):
-            swap_halves(ref, ch, yy)
-            return 0
-
-        lax.fori_loop(0, 8, step, 0)
+        def step(group, _):
+            for i in range(4):
+                swap_halves(ref, ch, 4 * group + i)
+            return 0
+
+        lax.fori_loop(0, 2, step, 0)
 
     def pair_walls():
         load_w.wait()
@@ -188,22 +191,17 @@
 
     def send_chunk(ch):
         load_f[ch].wait()
+        turn(ch)
         if ch == 0:
             pl.semaphore_wait(barrier, NT - 1 + NA - 1)
 
-        def step_t(i, _):
+        def step(i, _):
             for flip in (1, 0):
                 t = theta_peer(i, flip)
                 send(
                     t != th, F.at[pl.ds(2 * ch, 2), t], Qt.at[pl.ds(2 * ch, 2), pl.ds(TL * th, TL)],
                     sT.at[ch], rT.at[ch], (ax, t, grp),
                 )
-            return 0
-
-        lax.fori_loop(0, 8, step_t, 0)
-        turn(ch)
-
-        def step(i, _):
             yy = lax.rem(y + offset(i), 8)
             for g_to in range(2):
                 a_to = 4 * yy + g_to
@@ -451,14 +449,16 @@
         full(axh.at[ch], brX.at[ch])
         swap_all(axh, ch)
 
-        def add(x, _):
-            for cc in range(2):
-                c = 2 * ch + cc
-                axial = axh2[pl.ds(ch * 2 * XL * TL + cc * XL + x, TL, stride=2 * XL), :]
-                out[cc, x] = base[c, x] + cih[c, x] + axial
-            return 0
-
-        lax.fori_loop(0, XL, add, 0)
+        def add(group, _):
+            for i in range(4):
+                x = 4 * group + i
+                for cc in range(2):
+                    c = 2 * ch + cc
+                    axial = axh2[pl.ds(ch * 2 * XL * TL + cc * XL + x, TL, stride=2 * XL), :]
+                    out[cc, x] = base[c, x] + cih[c, x] + axial
+            return 0
+
+        lax.fori_loop(0, XL // 4, add, 0)
 
     gather(0, done)
     for c in range(2):

time: 61.2 us -> 60.7 us (level)
  no operation moved by 1% of the time
where the time goes in v6:
time: 60.7 us; the launch traced here: 60.6 us
  Pallas kernels  59.9 us (99%)
  between operations  0.64 us (1%)
    pallas_call x1, Pallas kernels, shards(): pl.pallas_call(kernel, out_shape=(buf(2, XL, TL, R), buf(2, XL, TL, R), b...  58.9 us

profile of v6, /device:TPU:1, one launch (start us, length us, event | category | flops | bytes accessed | tf_op | source)
XLA Modules:
  0.0 60.6 jit_solution(15847214774499129858)
XLA Ops:
  0.6 58.9 %shard_map.95 = (f32[2,16,24,128]{3,2,1,0:T(8,128)S(1)}, f32[2,16,24,128]{3,2,1,0:T(8,128)S(1)}, f32[16,24,64]{2,1,0:T(8,128)S(1)}, bf16[2,128,384]{2,1,0:T(8,128)(2,1)S(1)}) custom-call(f32[4,16,24,128]{3,2,1,0:T(8,128)} %fields_h.1, f32[16,24,64]{2,1,0:T(8,128)} %wall_h.1, f32[1,128]{1,0:T(1,128)} %bitcast.2, f32[2,128,128]{2,1,0:T(8,128)} %inv_h.1, ...), custom_call_target="tpu_custom_call" | custom-call | tf_op jit(solution)/shard_map/pallas_call | solution.py:543
  59.5 1.1 %shard_map.96 = (f32[4,16,24,128]{3,2,1,0:T(8,128)}, f32[16,24,64]{2,1,0:T(8,128)}) custom-call(f32[2,16,24,128]{3,2,1,0:T(8,128)S(1)} %get-tuple-element.6.done, f32[2,16,24,128]{3,2,1,0:T(8,128)S(1)} %get-tuple-element.7.rest, f32[16,24,64]{2,1,0:T(8,128)S(1)} %get-tuple-element.8.wdone, bf16[2,128,384]{2,1,0:T(8,128)(2,1)S(1)} %get-tuple-element.9.parts), custom_call_target="tpu_custom_call" | custom-call | tf_op jit(solution)/shard_map/pallas_call | solution.py:567

commit v7 on v6

--- a/solution.py
+++ b/solution.py
@@ -446,6 +446,14 @@
 
     def gather(ch, out):
         full(cih.at[pl.ds(2 * ch, 2)], brT.at[ch])
+
+        def add_circle(group, _):
+            for i in range(4):
+                for cc in range(2):
+                    out[cc, 4 * group + i] = base[2 * ch + cc, 4 * group + i] + cih[2 * ch + cc, 4 * group + i]
+            return 0
+
+        lax.fori_loop(0, XL // 4, add_circle, 0)
         full(axh.at[ch], brX.at[ch])
         swap_all(axh, ch)
 
@@ -453,9 +461,8 @@
             for i in range(4):
                 x = 4 * group + i
                 for cc in range(2):
-                    c = 2 * ch + cc
                     axial = axh2[pl.ds(ch * 2 * XL * TL + cc * XL + x, TL, stride=2 * XL), :]
-                    out[cc, x] = base[c, x] + cih[c, x] + axial
+                    out[cc, x] = out[cc, x] + axial
             return 0
 
         lax.fori_loop(0, XL // 4, add, 0)
@@ -522,10 +529,14 @@
     for copy in copies:
         copy.start()
     for c in range(2):
-        buf[c] = apply_inverse(parts[c], rest[c].reshape(XL * TL, R)).reshape(XL, TL, R)
-        copy = pltpu.make_async_copy(buf.at[c], out_h.at[2 + c], st.at[2 + c])
-        copy.start()
-        copies.append(copy)
+        for h in range(2):
+            rows = slice(h * XL // 2, (h + 1) * XL // 2)
+            value = rest[c, rows].reshape(XL * TL // 2, R)
+            buf[c, rows] = apply_inverse(parts[c], value).reshape(XL // 2, TL, R)
+            some = pl.ds(h * XL // 2, XL // 2)
+            copy = pltpu.make_async_copy(buf.at[c, some], out_h.at[2 + c, some], st.at[2 + 2 * c + h])
+            copy.start()
+            copies.append(copy)
     for copy in copies:
         copy.wait()
 
@@ -572,7 +583,7 @@
         ),
         in_specs=[vmem] * 4,
         out_specs=(hbm, hbm),
-        scratch_shapes=[buf(2, XL, TL, R), dma((4,))],
+        scratch_shapes=[buf(2, XL, TL, R), dma((6,))],
         compiler_params=pltpu.CompilerParams(vmem_limit_bytes=16 * 2**20),
     )(done, rest, wdone, parts)
 

time: 60.7 us -> 60.7 us (level)
  no operation moved by 1% of the time
where the time goes in v7:
time: 60.7 us; the launch traced here: 60.6 us
  Pallas kernels  59.9 us (99%)
  between operations  0.64 us (1%)
    pallas_call x1, Pallas kernels, shards(): pl.pallas_call(kernel, out_shape=(buf(2, XL, TL, R), buf(2, XL, TL, R), b...  58.9 us

profile of v7, /device:TPU:1, one launch (start us, length us, event | category | flops | bytes accessed | tf_op | source)
XLA Modules:
  0.0 60.6 jit_solution(7804415876286808190)
XLA Ops:
  0.6 58.9 %shard_map.95 = (f32[2,16,24,128]{3,2,1,0:T(8,128)S(1)}, f32[2,16,24,128]{3,2,1,0:T(8,128)S(1)}, f32[16,24,64]{2,1,0:T(8,128)S(1)}, bf16[2,128,384]{2,1,0:T(8,128)(2,1)S(1)}) custom-call(f32[4,16,24,128]{3,2,1,0:T(8,128)} %fields_h.1, f32[16,24,64]{2,1,0:T(8,128)} %wall_h.1, f32[1,128]{1,0:T(1,128)} %bitcast.2, f32[2,128,128]{2,1,0:T(8,128)} %inv_h.1, ...), custom_call_target="tpu_custom_call" | custom-call | tf_op jit(solution)/shard_map/pallas_call | solution.py:554
  59.6 1.0 %shard_map.96 = (f32[4,16,24,128]{3,2,1,0:T(8,128)}, f32[16,24,64]{2,1,0:T(8,128)}) custom-call(f32[2,16,24,128]{3,2,1,0:T(8,128)S(1)} %get-tuple-element.6.done, f32[2,16,24,128]{3,2,1,0:T(8,128)S(1)} %get-tuple-element.7.rest, f32[16,24,64]{2,1,0:T(8,128)S(1)} %get-tuple-element.8.wdone, bf16[2,128,384]{2,1,0:T(8,128)(2,1)S(1)} %get-tuple-element.9.parts), custom_call_target="tpu_custom_call" | custom-call | tf_op jit(solution)/shard_map/pallas_call | solution.py:578
